TPU v7x, 256 devices: a whole 4x4x8 slice. The times are simulated.
256 devices in a mesh: depth: 64 (over y, x, z_hi), tile: 4 (over z_lo, core).
Axes of the slice: x: 4, y: 4, z: 8 (z_hi: 4, z_lo: 2; z = z_hi * 2 + z_lo), core: 2. Of those that a mesh axis runs over, the one named last changes fastest.
Arguments:
- coarse: bfloat16 [128, 256, 256], P('depth', None, 'tile'), may hold values from -6 to 6
- residual: bfloat16 [256, 512, 512], P('depth', None, 'tile'), may hold values from -6 to 6
- levels: int32 [64, 128, 128], P('depth', None, 'tile'), may hold values from 0 to 2
- slab_rank: int32 [64], replicated, may hold values from -64 to 63, as said below
- light_angles: float32 [2], replicated, may hold values from -3.140625 to 3.140625
- color_slope: float32 [3], replicated, may hold values from 0.5 to 2
- color_shift: float32 [3], replicated, may hold values from -1 to 1
Outputs:
- image: float32 [4, 512, 512], P(None, 'depth', 'tile')
- slab_shade: float32 [64, 512, 512], P('depth', None, 'tile')
Inputs may be any that keep to these rules, and one draw needn't show every extreme that they name: With p = s for every slab s, or p = 63 - s for every slab s, and one whole number c of 1 to 32: slab_rank is p where p >= c and p - 64 where p < c.
All inputs are finite; a program needn't handle non-finite values.
Results may differ from a plain program's by a relative error of at most 0.00079.
Values may be sent and summed in bfloat16 or wider, within the bound.
No kernel may reach another device: no remote copies, remote signals or barrier semaphores. Data moves between devices by JAX's collectives and lax.ppermute only.
A program may use at most 192 MiB of HBM per device.

v0:
```python
import jax
import jax.numpy as jnp
from jax import lax
from jax.sharding import PartitionSpec as P


def padded_2(shard, sides, width):
    edges = {}
    for axis, dim in sides:
        count, length = (lax.axis_size(axis), shard.shape[dim])
        up = [(i, (i + 1) % count) for i in range(count - 1)]
        last = lax.slice_in_dim(shard, length - width, length, axis=dim)
        initial = lax.slice_in_dim(shard, 0, width, axis=dim)
        edges[dim] = (
            lax.ppermute(last, axis, up),
            lax.ppermute(initial, axis, [(b, a) for a, b in up]),
        )
    done = []
    for _, dim in sides:
        low, high = edges[dim]
        around = [(width, width) if d in done else (0, 0) for d in range(shard.ndim)]
        shard = jnp.concatenate([jnp.pad(low, around), shard, jnp.pad(high, around)], axis=dim)
        done.append(dim)
    return shard


def refine_block(coarse_part, residual_part, level_part):
    dep, rows, cols = residual_part.shape
    lifted = coarse_part.astype(jnp.float32)[:, None, :, None, :, None]
    lifted = jnp.broadcast_to(lifted, (dep // 2, 2, rows // 2, 2, cols // 2, 2)).reshape(
        dep, rows, cols
    )
    nb = level_part.shape
    scaled = level_part.astype(jnp.float32)[:, None, :, None, :, None]
    scaled = jnp.broadcast_to(
        scaled, (nb[0], dep // nb[0], nb[1], rows // nb[1], nb[2], cols // nb[2])
    ).reshape(dep, rows, cols)
    return (lifted + 0.5 * scaled * residual_part.astype(jnp.float32)).astype(jnp.bfloat16)


def light_vector(angles):
    return jnp.stack(
        [
            jnp.sin(angles[1]),
            jnp.cos(angles[1]) * jnp.sin(angles[0]),
            jnp.cos(angles[1]) * jnp.cos(angles[0]),
        ]
    )


def render_slab(padded, ascending, step, light, slope, shift):
    f = padded.astype(jnp.float32)
    v = f[2:-2, 2:-2, 2:-2]
    grad_z = (
        f[:-4, 2:-2, 2:-2]
        - 8.0 * f[1:-3, 2:-2, 2:-2]
        + 8.0 * f[3:-1, 2:-2, 2:-2]
        - f[4:, 2:-2, 2:-2]
    ) / 12.0
    grad_y = (
        f[2:-2, :-4, 2:-2]
        - 8.0 * f[2:-2, 1:-3, 2:-2]
        + 8.0 * f[2:-2, 3:-1, 2:-2]
        - f[2:-2, 4:, 2:-2]
    ) / 12.0
    grad_x = (
        f[2:-2, 2:-2, :-4]
        - 8.0 * f[2:-2, 2:-2, 1:-3]
        + 8.0 * f[2:-2, 2:-2, 3:-1]
        - f[2:-2, 2:-2, 4:]
    ) / 12.0
    along = light[0] * grad_z + light[1] * grad_y + light[2] * grad_x
    shade = 0.25 + 0.75 * jnp.abs(along) / jnp.sqrt(
        grad_z * grad_z + grad_y * grad_y + grad_x * grad_x + 1.0
    )
    extinct = 4.0 * jax.nn.sigmoid(3.0 * (v - 1.5))
    running = jnp.cumsum(extinct, axis=0)
    total = running[-1]
    before = jnp.where(ascending, running - extinct, total - running)
    weight = jnp.exp(-step * before) * (1.0 - jnp.exp(-step * extinct)) * shade
    colors = [jnp.sum(weight * jax.nn.sigmoid(slope[k] * v + shift[k]), axis=0) for k in range(3)]
    return (jnp.stack(colors + [1.0 - jnp.exp(-step * total)]), jnp.mean(shade, axis=0))


def shards(coarse, residual, levels, slab_rank, light_angles, color_slope, color_shift):
    dep, rows, cols = residual.shape
    slabs = lax.axis_size("depth")
    me = lax.axis_index("depth")
    ascending = slab_rank[0] < slab_rank[slabs - 1]
    my_rank = lax.dynamic_index_in_dim(slab_rank, me, 0, keepdims=False)
    visible = (my_rank >= 0).astype(jnp.float32)
    refined = refine_block(coarse, residual, levels)
    padded = padded_2(refined, (("depth", 0), ("tile", 2)), 2)
    padded = jnp.pad(padded, ((0, 0), (2, 2), (0, 0)))
    step = 4.0 / (dep * slabs)
    slab_image, mean_shade = render_slab(
        padded, ascending, step, light_vector(light_angles), color_slope, color_shift
    )
    slab_image = slab_image * visible
    shade_block = mean_shade[None]
    row_dev = rows // slabs
    blocks = slab_image.reshape(4, slabs, row_dev, cols)
    received = lax.all_to_all(blocks, "depth", split_axis=1, concat_axis=1, tiled=True)
    ordered = jnp.where(ascending, received, jnp.flip(received, 1))
    clear = jnp.cumprod(1.0 - ordered[3:4], axis=1)
    through = jnp.concatenate([jnp.ones_like(clear[:, :1]), clear[:, :-1]], axis=1)
    composed = jnp.sum(through * ordered, axis=1)
    return (composed, shade_block)


def solution(mesh):
    placed = (
        P("depth", None, "tile"),
        P("depth", None, "tile"),
        P("depth", None, "tile"),
        P(),
        P(),
        P(),
        P(),
    )
    return jax.shard_map(
        shards,
        mesh=mesh,
        in_specs=placed,
        out_specs=(P(None, "depth", "tile"), P("depth", None, "tile")),
        check_vma=False,
    )
```

profile of v0, /device:TPU:1, one launch (start us, length us, event | category | flops | bytes accessed | tf_op | source)
XLA Modules:
  0.0 165.1 jit_solution(7938170140834256368)
XLA Ops:
  0.6 0.9 copy.13
  1.6 21.6 %broadcast_in_dim.6 = f32[2,2,256,2,64,2]{5,4,3,2,1,0:T(8,128)} broadcast(f32[2,256,64]{2,1,0:T(8,128)S(1)} %copy.13), dimensions={0,2,4} | broadcast | bytes 1179648 | tf_op jit(solution)/shard_map/broadcast_in_dim | solution.py:30
  23.2 46.8 %reshape.51 = f32[4,512,128]{2,1,0:T(8,128)S(1)} reshape(f32[2,2,256,2,64,2]{5,4,3,2,1,0:T(8,128)} %broadcast_in_dim.6) | data formatting | bytes 2097152 | tf_op jit(solution)/shard_map/reshape | solution.py:30
  70.0 0.1 copy.14
  70.1 3.8 %broadcast_in_dim.7 = f32[128,4,32,4]{3,2,1,0:T(8,128)} broadcast(f32[128,32]{1,0:T(8,128)S(1)} %copy.14), dimensions={0,2} | broadcast | bytes 278528 | tf_op jit(solution)/shard_map/broadcast_in_dim | solution.py:35
  73.9 8.2 %mul.170 = f32[512,128]{1,0:T(8,128)S(1)} reshape(f32[128,4,32,4]{3,2,1,0:T(8,128)} %broadcast_in_dim.7) | data formatting | bytes 524288 | tf_op jit(solution)/shard_map/mul | solution.py:38
  82.2 0.0 copy-start.3
  82.2 0.1 add_convert_fusion
  82.4 0.2 fusion.24
  82.6 4.9 %collective-permute-start = (bf16[4,512,2]{2,1,0:T(8,128)(2,1)S(1)}, bf16[4,512,2]{2,1,0:T(8,128)(2,1)S(1)}, u32[]{:S(2)}, u32[]{:S(2)}) collective-permute-start(bf16[4,512,2]{2,1,0:T(8,128)(2,1)S(1)} %get-tuple-element.11), channel_id=1, source_target_pairs={{0,1},{1,2},{2,3},{4,5},{5,6},{6,7},{8,9},{9,10},{10,11},{12,13},{... | collective-permute-start | bytes 24584 | tf_op jit(solution)/shard_map/ppermute | solution.py:15
  87.5 1.9 %collective-permute-start.3 = (bf16[4,512,2]{2,1,0:T(8,128)(2,1)S(1)}, bf16[4,512,2]{2,1,0:T(8,128)(2,1)S(1)}, u32[]{:S(2)}, u32[]{:S(2)}) collective-permute-start(bf16[4,512,2]{2,1,0:T(8,128)(2,1)S(1)} %get-tuple-element.12), channel_id=1, source_target_pairs={{1,0},{2,1},{3,2},{5,4},{6,5},{7,6},{9,8},{10,9},{11,10},{13,12},{... | collective-permute-start | bytes 24584 | tf_op jit(solution)/shard_map/ppermute | solution.py:16
  89.4 0.7 fusion.23
  90.2 4.9 %collective-permute-start.1 = (bf16[2,512,128]{2,1,0:T(8,128)(2,1)}, bf16[2,512,128]{2,1,0:T(8,128)(2,1)S(1)}, u32[]{:S(2)}, u32[]{:S(2)}) collective-permute-start(bf16[2,512,128]{2,1,0:T(8,128)(2,1)} %get-tuple-element.9), channel_id=1, source_target_pairs={{0,4},{4,8},{8,12},{12,16},{16,20},{20,24},{24,28},{28,32},{32,36}... | collective-permute-start | bytes 786440 | tf_op jit(solution)/shard_map/ppermute | solution.py:15
  95.1 1.3 collective-permute-start.2
  96.4 0.6 fusion.27
  97.0 0.6 fusion.26
  97.7 0.7 fusion.25
  98.3 0.6 fusion.28
  103.7 7.8 %collective-permute-done.2 = bf16[2,512,128]{2,1,0:T(8,128)(2,1)S(1)} collective-permute-done((bf16[2,512,128]{2,1,0:T(8,128)(2,1)S(1)}, bf16[2,512,128]{2,1,0:T(8,128)(2,1)S(1)}, u32[]{:S(2)}, u32[]{:S(2)}) %collective-permute-start.2) | collective-permute-done | bytes 262176 | tf_op jit(solution)/shard_map/ppermute | solution.py:16
  111.5 1.6 fusion.2
  113.1 0.5 pad_convert_fusion
  113.6 0.5 fusion.10
  114.0 0.1 slice_bitcast_fusion
  114.1 3.2 %fusion.22 = (f32[512,128]{1,0:T(8,128)S(1)}, f32[4,512,128]{2,1,0:T(8,128)S(1)}) fusion(f32[]{:T(128)} %bitcast.5, f32[8,516,132]{2,1,0:T(8,128)S(1)} %pad_convert_fusion, f32[]{:T(128)} %bitcast.4, f32[]{:T(128)} %bitcast.3), kind=kLoop, calls=%fused_computation.49 | loop fusion | flops 8847360 | bytes 13893644 | tf_op jit(solution)/shard_map/reduce_sum | solution.py:82
  117.3 5.4 %multiply_reduce_fusion.3 = (f32[512,128]{1,0:T(8,128)S(1)}, f32[512,128]{1,0:T(8,128)S(1)}, f32[512,128]{1,0:T(8,128)S(1)}) fusion(f32[8,516,132]{2,1,0:T(8,128)S(1)} %pad_convert_fusion, f32[]{:T(128)} %bitcast.7, f32[]{:T(128)} %bitcast.6, f32[]{:T(128)} %bitcast.13, f32[]{:T(128)} %bitcast.12, f32[]{:T(128)} %bitcast.10, f32[]{:T(128)} %bitcast.9, ...), kind=kLoop, calls=%fused_computation.27 | loop fusion | flops 8978432 | bytes 4194329 | tf_op jit(solution)/shard_map/reduce_sum | solution.py:81
  122.7 1.1 maximum_multiply_fusion
  123.8 11.2 %all-to-all-start = ((f32[4,64,8,128]{3,2,0,1:T(8,128)}), f32[4,64,8,128]{3,2,0,1:T(8,128)S(1)}, u32[]{:S(2)}, u32[]{:S(2)}) async-start(f32[4,64,8,128]{3,2,0,1:T(8,128)} %maximum_multiply_fusion), calls=%async_computation | async-start | bytes 2097152 | tf_op jit(solution)/shard_map/all_to_all | solution.py:103
  135.0 0.7 multiply_bitcast_fusion
  135.7 28.3 %all-to-all-done = f32[4,64,8,128]{3,2,0,1:T(8,128)S(1)} async-done(((f32[4,64,8,128]{3,2,0,1:T(8,128)}), f32[4,64,8,128]{3,2,0,1:T(8,128)S(1)}, u32[]{:S(2)}, u32[]{:S(2)}) %all-to-all-start) | async-done | bytes 1048608 | tf_op jit(solution)/shard_map/all_to_all | solution.py:103
  164.1 0.1 reverse_select_fusion
  164.2 0.1 fusion.14
  164.3 0.8 multiply_reduce_fusion
  (17 shorter events, 0.1 us)
Async XLA Ops:
  23.1 46.8 %copy-start.1 = (s32[1,128,32]{1,2,0:T(8,128)S(1)}, s32[1,128,32]{1,2,0:T(8,128)}, u32[]{:S(2)}) copy-start(s32[1,128,32]{1,2,0:T(8,128)} %param.9) | copy-start | bytes 49156
  73.9 8.2 %copy-start = (bf16[4,512,128]{2,1,0:T(8,128)(2,1)S(1)}, bf16[4,512,128]{2,1,0:T(8,128)(2,1)}, u32[]{:S(2)}) copy-start(bf16[4,512,128]{2,1,0:T(8,128)(2,1)} %param.8) | copy-start | bytes 1572868
  82.2 14.2 %copy-start.3 = (f32[3]{0:T(128)S(1)}, f32[3]{0:T(128)}, u32[]{:S(2)}) copy-start(f32[3]{0:T(128)} %param.13) | copy-start | bytes 40
  82.2 14.8 %copy-start.4 = (f32[3]{0:T(128)S(1)}, f32[3]{0:T(128)}, u32[]{:S(2)}) copy-start(f32[3]{0:T(128)} %param.12) | copy-start | bytes 40
  82.2 15.5 %copy-start.2 = (s32[64]{0:T(128)S(1)}, s32[64]{0:T(128)}, u32[]{:S(2)}) copy-start(s32[64]{0:T(128)} %param.10) | copy-start | bytes 772
  82.2 16.1 %copy-start.5 = (f32[2]{0:T(128)S(1)}, f32[2]{0:T(128)}, u32[]{:S(2)}) copy-start(f32[2]{0:T(128)} %param.11) | copy-start | bytes 28
  82.6 21.1 %collective-permute-start = (bf16[4,512,2]{2,1,0:T(8,128)(2,1)S(1)}, bf16[4,512,2]{2,1,0:T(8,128)(2,1)S(1)}, u32[]{:S(2)}, u32[]{:S(2)}) collective-permute-start(bf16[4,512,2]{2,1,0:T(8,128)(2,1)S(1)} %get-tuple-element.11), channel_id=1, source_target_pairs={{0,1},{1,2},{2,3},{4,5},{5,6},{6,7},{8,9},{9,10},{10,11},{12,13},{... | collective-permute-start | bytes 24584 | tf_op jit(solution)/shard_map/ppermute | solution.py:15
  87.5 16.2 %collective-permute-start.3 = (bf16[4,512,2]{2,1,0:T(8,128)(2,1)S(1)}, bf16[4,512,2]{2,1,0:T(8,128)(2,1)S(1)}, u32[]{:S(2)}, u32[]{:S(2)}) collective-permute-start(bf16[4,512,2]{2,1,0:T(8,128)(2,1)S(1)} %get-tuple-element.12), channel_id=1, source_target_pairs={{1,0},{2,1},{3,2},{5,4},{6,5},{7,6},{9,8},{10,9},{11,10},{13,12},{... | collective-permute-start | bytes 24584 | tf_op jit(solution)/shard_map/ppermute | solution.py:16
  90.2 13.5 %collective-permute-start.1 = (bf16[2,512,128]{2,1,0:T(8,128)(2,1)}, bf16[2,512,128]{2,1,0:T(8,128)(2,1)S(1)}, u32[]{:S(2)}, u32[]{:S(2)}) collective-permute-start(bf16[2,512,128]{2,1,0:T(8,128)(2,1)} %get-tuple-element.9), channel_id=1, source_target_pairs={{0,4},{4,8},{8,12},{12,16},{16,20},{20,24},{24,28},{28,32},{32,36}... | collective-permute-start | bytes 786440 | tf_op jit(solution)/shard_map/ppermute | solution.py:15
  95.1 16.5 %collective-permute-start.2 = (bf16[2,512,128]{2,1,0:T(8,128)(2,1)S(1)}, bf16[2,512,128]{2,1,0:T(8,128)(2,1)S(1)}, u32[]{:S(2)}, u32[]{:S(2)}) collective-permute-start(bf16[2,512,128]{2,1,0:T(8,128)(2,1)S(1)} %get-tuple-element.10), channel_id=1, source_target_pairs={{4,0},{8,4},{12,8},{16,12},{20,16},{24,20},{28,24},{32,28},{36,32}... | collective-permute-start | bytes 786440 | tf_op jit(solution)/shard_map/ppermute | solution.py:16
  123.8 40.3 %all-to-all-start = ((f32[4,64,8,128]{3,2,0,1:T(8,128)}), f32[4,64,8,128]{3,2,0,1:T(8,128)S(1)}, u32[]{:S(2)}, u32[]{:S(2)}) async-start(f32[4,64,8,128]{3,2,0,1:T(8,128)} %maximum_multiply_fusion), calls=%async_computation | async-start | bytes 2097152 | tf_op jit(solution)/shard_map/all_to_all | solution.py:103
where the time goes:
time: 168 us; the launch traced here: 165 us
  local copies, waits for them, and re-layouts  85.1 us (51%)
  waiting for transfers between devices  36.1 us (21%)
  starting transfers between devices  24.3 us (14%)
  other arithmetic  14 us (8%)
  between operations  5.58 us (3%)
    reshape x1, local copies, waits for them, and re-layouts, refine_block(): jnp.broadcast_to(lifted, (dep // 2, 2, rows // 2, 2, cols // 2, 2))  46.8 us
    all_to_all x1, waiting for transfers between devices, shards(): lax.all_to_all(blocks, 'depth', split_axis=1, concat_axis=1, tiled=True)  28.3 us
    broadcast_in_dim x1, local copies, waits for them, and re-layouts, refine_block(): jnp.broadcast_to(lifted, (dep // 2, 2, rows // 2, 2, cols // 2, 2))  21.6 us
    all_to_all x1, starting transfers between devices, shards(): lax.all_to_all(blocks, 'depth', split_axis=1, concat_axis=1, tiled=True)  11.2 us
    ppermute x2, starting transfers between devices, padded_2(): lax.ppermute(last, axis, up)  9.82 us
    mul x2, local copies, waits for them, and re-layouts, refine_block(): 0.5 * scaled * residual_part.astype(jnp.float32)  8.32 us
    ppermute x2, waiting for transfers between devices, padded_2(): lax.ppermute(initial, axis, [(b, a) for a, b in up])  7.81 us
    reduce_sum x1, other arithmetic, render_slab(): jnp.sum(weight * jax.nn.sigmoid(slope[k] * v + shift[k]), axis=0)  5.41 us
  transfers between devices with their start and end apart: 5, of which 2 were waited for; matrix products, arithmetic and copies ran while one was open for 2% of the time, Pallas kernels for 0%

commit v1 on v0

v1 whole, which is shorter than its diff:
```python
import jax
import jax.numpy as jnp
from jax import lax
from jax.experimental import pallas as pl
from jax.experimental.pallas import tpu as pltpu
from jax.sharding import PartitionSpec as P

F32 = jnp.float32
BF16 = jnp.bfloat16
VMEM = pl.BlockSpec(memory_space=pltpu.VMEM)
SMEM = pl.BlockSpec(memory_space=pltpu.SMEM)
NN = (((1,), (0,)), ((), ()))
NT = (((1,), (1,)), ((), ()))
PAD = 64
BLK = 128
SUB = 16


def dot(a, b, dims=NN):
    return lax.dot_general(a, b, dims, preferred_element_type=F32)


def iota2(shape):
    return (
        lax.broadcasted_iota(jnp.int32, shape, 0),
        lax.broadcasted_iota(jnp.int32, shape, 1),
    )


def repeater(out, inner):
    r, c = iota2((out, inner))
    return jnp.where(r // (out // inner) == c, 1.0, 0.0).astype(BF16)


def stencil(offset):
    w = jnp.where(offset == -2, 1.0, jnp.where(offset == -1, -8.0, 0.0))
    return jnp.where(offset == 1, 8.0, jnp.where(offset == 2, -1.0, w))


def refine_kernel(res_ref, coarse_ref, level_ref, low_ref, high_ref, up_ref, down_ref):
    dep, rows, cols = res_ref.shape
    half = coarse_ref.shape[2]
    widen2 = repeater(cols, coarse_ref.shape[1])
    widen4 = repeater(cols, level_ref.shape[0])
    lev = dot(widen4, level_ref[...].astype(F32).astype(BF16)).astype(BF16)
    scale = 0.5 * dot(repeater(rows, lev.shape[1]), lev, NT)
    tall2 = repeater(256, 128)
    k, c = iota2((16, cols))
    edges = jnp.zeros((16, rows), F32)
    for zc in range(dep // 2):
        wide = dot(widen2, coarse_ref[zc]).astype(BF16)
        lifted = [dot(tall2, wide[:, b * 128 : (b + 1) * 128], NT) for b in range(half // 128)]
        for z in (2 * zc, 2 * zc + 1):
            out = low_ref if z < 2 else high_ref
            for b in range(half // 128):
                part = pl.ds(b * 256, 256)
                out[z % 2, part, :] = (
                    lifted[b] + scale[b * 256 : (b + 1) * 256] * res_ref[z, part, :].astype(F32)
                ).astype(BF16)
            col = jnp.where(k < 8, k - 2 * z + cols - 2, k - 8 - 2 * z)
            mine = (k % 8) // 2 == z
            pick = jnp.where(mine & (col == c), 1.0, 0.0).astype(BF16)
            edges = edges + dot(pick, out[z % 2], NT)
    up_ref[...] = edges[0:8].astype(BF16)
    down_ref[...] = edges[8:16].astype(BF16)


def refine(residual, coarse, levels):
    dep, rows, cols = residual.shape
    plane = jax.ShapeDtypeStruct((dep // 2, rows, cols), BF16)
    edge = jax.ShapeDtypeStruct((2 * dep, rows), BF16)
    return pl.pallas_call(
        refine_kernel,
        out_shape=(plane, plane, edge, edge),
        in_specs=[VMEM] * 3,
        out_specs=(VMEM,) * 4,
        name="refine",
    )(residual, jnp.swapaxes(coarse, 1, 2), jnp.swapaxes(levels[0], 0, 1))


def render_kernel(
    step, low_ref, high_ref, before_ref, after_ref, left_ref, right_ref,
    rank_ref, angle_ref, slope_ref, shift_ref, image_ref, shade_ref, pair, gx_ref, gy_ref,
):
    _, rows, cols = low_ref.shape
    slabs = rank_ref.shape[0]
    ascending = rank_ref[0] < rank_ref[slabs - 1]
    visible = jnp.where(rank_ref[lax.axis_index("depth")] >= 0, 1.0, 0.0).astype(F32)
    azimuth = jnp.full((SUB, cols), angle_ref[0], F32)
    elevation = jnp.full((SUB, cols), angle_ref[1], F32)
    light_z = jnp.sin(elevation)
    light_y = jnp.cos(elevation) * jnp.sin(azimuth)
    light_x = jnp.cos(elevation) * jnp.cos(azimuth)
    slope = [0.5 * slope_ref[k] for k in range(3)]
    shift = [0.5 * shift_ref[k] for k in range(3)]

    zero = jnp.zeros((PAD, 2 * cols), BF16)
    for p, ref in enumerate((low_ref, high_ref)):
        pair[p, 0:PAD, :] = zero
        pair[p, PAD + rows :, :] = zero
        for q in range(2):
            pair[p, PAD : PAD + rows, q * cols : (q + 1) * cols] = ref[q]

    r, c = iota2((cols, cols))
    across = stencil(r - c).astype(BF16)
    r, c = iota2((BLK, BLK + 2 * PAD))
    along = stencil(c - PAD - r).astype(BF16)
    k, c = iota2((16, cols))
    spot = jnp.where(k < 8, k % 2 - 2, cols + k % 2)
    beside = [
        jnp.where((k % 8) // 2 == z, stencil(spot - c), 0.0).astype(BF16) for z in range(4)
    ]
    columns = jnp.concatenate([left_ref[...].astype(F32), right_ref[...].astype(F32)], 0)
    columns = columns.T.astype(BF16)

    for b in range(rows // BLK):
        base = b * BLK
        for p, ref in enumerate((low_ref, high_ref)):
            gy_ref[p] = dot(along, pair[p, base : base + BLK + 2 * PAD, :])
            for q in range(2):
                gx_ref[2 * p + q] = dot(ref[q, base : base + BLK, :], across) + dot(
                    columns[base : base + BLK], beside[2 * p + q]
                )

        def shade_rows(i, carry, base=base):
            at = pl.ds(pl.multiple_of(i * SUB, SUB), SUB)
            row = pl.ds(pl.multiple_of(base + i * SUB, SUB), SUB)
            planes = [
                ref[q, row, :].astype(F32)
                for ref in (before_ref, low_ref, high_ref, after_ref)
                for q in range(2)
            ]
            clear, alpha, shade, color = [], [], [], []
            for z in range(4):
                v = planes[z + 2]
                gz = (planes[z] - planes[z + 4]) + 8.0 * (planes[z + 3] - planes[z + 1])
                gy = gy_ref[z // 2, at, (z % 2) * cols : (z % 2 + 1) * cols]
                gx = gx_ref[z, at, :]
                lit = light_z * gz + light_y * gy + light_x * gx
                size = gz * gz + gy * gy + gx * gx + 144.0
                shade.append(0.25 + 0.75 * (jnp.abs(lit) * lax.rsqrt(size)))
                extinct = 2.0 + 2.0 * jnp.tanh(1.5 * v - 2.25)
                clear.append(jnp.exp(-step * extinct))
                alpha.append((1.0 - clear[z]) * shade[z])
                color.append([0.5 + 0.5 * jnp.tanh(slope[n] * v + shift[n]) for n in range(3)])
            up = [None, clear[0], clear[0] * clear[1], None]
            up[3] = up[2] * clear[2]
            down = [None, None, clear[3], None]
            down[1] = clear[3] * clear[2]
            down[0] = down[1] * clear[1]
            before = [
                jnp.where(ascending, 1.0, down[0]),
                jnp.where(ascending, up[1], down[1]),
                jnp.where(ascending, up[2], down[2]),
                jnp.where(ascending, up[3], 1.0),
            ]
            weight = [before[z] * alpha[z] * visible for z in range(4)]
            out = [
                (weight[0] * color[0][n] + weight[1] * color[1][n])
                + (weight[2] * color[2][n] + weight[3] * color[3][n])
                for n in range(3)
            ]
            out.append((1.0 - up[3] * clear[3]) * visible)
            for half in range(SUB // 8):
                tile = jnp.concatenate([x[half * 8 : half * 8 + 8] for x in out], 0)
                image_ref[(base // 8) + i * (SUB // 8) + half] = tile.astype(image_ref.dtype)
            shade_ref[0, row, :] = 0.25 * ((shade[0] + shade[1]) + (shade[2] + shade[3]))
            return carry

        lax.fori_loop(0, BLK // SUB, shade_rows, 0, unroll=2)


def render(step, low, high, before, after, left, right, rank, angles, slope, shift):
    _, rows, cols = low.shape
    return pl.pallas_call(
        lambda *refs: render_kernel(step, *refs),
        out_shape=(
            jax.ShapeDtypeStruct((rows // 8, 32, cols), BF16),
            jax.ShapeDtypeStruct((1, rows, cols), F32),
        ),
        in_specs=[VMEM] * 6 + [SMEM] * 4,
        out_specs=(VMEM, VMEM),
        scratch_shapes=[
            pltpu.VMEM((2, rows + 2 * PAD, 2 * cols), BF16),
            pltpu.VMEM((4, BLK, cols), F32),
            pltpu.VMEM((2, BLK, 2 * cols), F32),
        ],
        name="render",
    )(low, high, before, after, left, right, rank, angles, slope, shift)


def compose_kernel(part_ref, rank_ref, image_ref):
    slabs = part_ref.shape[0]
    cols = part_ref.shape[2]
    ascending = rank_ref[0] < rank_ref[slabs - 1]

    def body(i, carry):
        through, red, green, blue = carry
        tile = part_ref[jnp.where(ascending, i, slabs - 1 - i)].astype(F32)
        red = red + through * tile[0:8]
        green = green + through * tile[8:16]
        blue = blue + through * tile[16:24]
        return (through * (1.0 - tile[24:32]), red, green, blue)

    zero = jnp.zeros((8, cols), F32)
    through, red, green, blue = lax.fori_loop(
        0, slabs, body, (jnp.ones((8, cols), F32), zero, zero, zero), unroll=8
    )
    image_ref[0] = red
    image_ref[1] = green
    image_ref[2] = blue
    image_ref[3] = 1.0 - through


def compose(parts, rank):
    return pl.pallas_call(
        compose_kernel,
        out_shape=jax.ShapeDtypeStruct((4, 8, parts.shape[2]), F32),
        in_specs=[VMEM, SMEM],
        out_specs=VMEM,
        name="compose",
    )(parts, rank)


def shards(coarse, residual, levels, slab_rank, light_angles, color_slope, color_shift):
    dep = residual.shape[0]
    slabs, tiles = lax.axis_size("depth"), lax.axis_size("tile")
    step = 4.0 / (dep * slabs)
    low, high, up, down = refine(residual, coarse, levels)
    fore = lambda n: [(i, i + 1) for i in range(n - 1)]
    back = lambda n: [(i + 1, i) for i in range(n - 1)]
    before = lax.ppermute(high, "depth", fore(slabs))
    after = lax.ppermute(low, "depth", back(slabs))
    left = lax.ppermute(up, "tile", fore(tiles))
    right = lax.ppermute(down, "tile", back(tiles))
    image, shade = render(
        step, low, high, before, after, left, right,
        slab_rank, light_angles, color_slope, color_shift,
    )
    parts = lax.all_to_all(image, "depth", split_axis=0, concat_axis=0, tiled=True)
    return (compose(parts, slab_rank), shade)


def solution(mesh):
    placed = (
        P("depth", None, "tile"),
        P("depth", None, "tile"),
        P("depth", None, "tile"),
        P(),
        P(),
        P(),
        P(),
    )
    return jax.shard_map(
        shards,
        mesh=mesh,
        in_specs=placed,
        out_specs=(P(None, "depth", "tile"), P("depth", None, "tile")),
        check_vma=False,
    )
```

time: 168 us -> 66.8 us (0.40)
  the two profiles are of different devices: /device:TPU:1 before, /device:TPU:32 now
where the time goes in v1:
time: 66.8 us; the launch traced here: 66.5 us
  blocking collectives  37.2 us (56%)
  starting transfers between devices  12.7 us (19%)
  Pallas kernels  9.71 us (15%)
  waiting for transfers between devices  5.46 us (8%)
  local copies, waits for them, and re-layouts  0.72 us (1%)
  between operations  0.69 us (1%)
    all_to_all x1, blocking collectives, shards(): lax.all_to_all(image, 'depth', split_axis=0, concat_axis=0, tiled=True)  37.2 us
    ppermute x1, starting transfers between devices, shards(): before = lax.ppermute(high, 'depth', fore(slabs))  5.82 us
    pallas_call x1, Pallas kernels, render(): pl.pallas_call(lambda *refs: render_kernel(step, *refs), out_shape=(jax.S...  5.3 us
    ppermute x1, waiting for transfers between devices, shards(): before = lax.ppermute(high, 'depth', fore(slabs))  3.92 us
    ppermute x1, starting transfers between devices, shards(): right = lax.ppermute(down, 'tile', back(tiles))  3.64 us
    pallas_call x1, Pallas kernels, refine(): pl.pallas_call(refine_kernel, out_shape=(plane, plane, edge, edge), in_sp...  2.59 us
    ppermute x1, starting transfers between devices, shards(): left = lax.ppermute(up, 'tile', fore(tiles))  1.92 us
    pallas_call x1, Pallas kernels, compose(): pl.pallas_call(compose_kernel, out_shape=jax.ShapeDtypeStruct((4, 8, part...  1.82 us
  transfers between devices with their start and end apart: 4, of which 2 were waited for; matrix products, arithmetic and copies ran while one was open for 0% of the time, Pallas kernels for 0%

profile of v1, /device:TPU:32, one launch (start us, length us, event | category | flops | bytes accessed | tf_op | source)
XLA Modules:
  0.0 66.5 jit_solution(10249142734922558944)
XLA Ops:
  0.6 2.6 %refine.1 = (bf16[2,512,128]{2,1,0:T(8,128)(2,1)}, bf16[2,512,128]{2,1,0:T(8,128)(2,1)}, bf16[8,512]{1,0:T(8,128)(2,1)}, bf16[8,512]{1,0:T(8,128)(2,1)}) custom-call(bf16[4,512,128]{2,1,0:T(8,128)(2,1)} %res_ref.1, bf16[2,64,256]{2,1,0:T(8,128)(2,1)} %bitcast.4, s32[32,128]{1,0:T(8,128)} %bitcast.5), custom_call_target="tpu_custom_call" | custom-call | tf_op jit(solution)/shard_map/refine/pallas_call | solution.py:72
  3.2 1.3 %collective-permute-start.1 = (bf16[2,512,128]{2,1,0:T(8,128)(2,1)}, bf16[2,512,128]{2,1,0:T(8,128)(2,1)S(1)}, u32[]{:S(2)}, u32[]{:S(2)}) collective-permute-start(bf16[2,512,128]{2,1,0:T(8,128)(2,1)} %get-tuple-element.8.refs_0_), channel_id=1, source_target_pairs={{4,0},{8,4},{12,8},{16,12},{20,16},{24,20},{28,24},{32,28},{36,32}... | collective-permute-start | bytes 786440 | tf_op jit(solution)/shard_map/ppermute | solution.py:233
  4.5 5.8 %collective-permute-start = (bf16[2,512,128]{2,1,0:T(8,128)(2,1)}, bf16[2,512,128]{2,1,0:T(8,128)(2,1)S(1)}, u32[]{:S(2)}, u32[]{:S(2)}) collective-permute-start(bf16[2,512,128]{2,1,0:T(8,128)(2,1)} %get-tuple-element.9.refs_1_), channel_id=1, source_target_pairs={{0,4},{4,8},{8,12},{12,16},{16,20},{20,24},{24,28},{28,32},{32,36}... | collective-permute-start | bytes 786440 | tf_op jit(solution)/shard_map/ppermute | solution.py:232
  10.3 1.9 %collective-permute-start.2 = (bf16[8,512]{1,0:T(8,128)(2,1)}, bf16[8,512]{1,0:T(8,128)(2,1)S(1)}, u32[]{:S(2)}, u32[]{:S(2)}) collective-permute-start(bf16[8,512]{1,0:T(8,128)(2,1)} %get-tuple-element.10), channel_id=1, source_target_pairs={{0,1},{1,2},{2,3},{4,5},{5,6},{6,7},{8,9},{9,10},{10,11},{12,13},{... | collective-permute-start | bytes 24584 | tf_op jit(solution)/shard_map/ppermute | solution.py:234
  12.3 3.6 %collective-permute-start.3 = (bf16[8,512]{1,0:T(8,128)(2,1)}, bf16[8,512]{1,0:T(8,128)(2,1)S(1)}, u32[]{:S(2)}, u32[]{:S(2)}) collective-permute-start(bf16[8,512]{1,0:T(8,128)(2,1)} %get-tuple-element.11), channel_id=1, source_target_pairs={{1,0},{2,1},{3,2},{5,4},{6,5},{7,6},{9,8},{10,9},{11,10},{13,12},{... | collective-permute-start | bytes 24584 | tf_op jit(solution)/shard_map/ppermute | solution.py:235
  15.9 0.0 collective-permute-done.2.refs_4_
  15.9 0.0 copy-start.2
  15.9 1.5 %collective-permute-done.3.refs_5_ = bf16[8,512]{1,0:T(8,128)(2,1)S(1)} collective-permute-done((bf16[8,512]{1,0:T(8,128)(2,1)}, bf16[8,512]{1,0:T(8,128)(2,1)S(1)}, u32[]{:S(2)}, u32[]{:S(2)}) %collective-permute-start.3) | collective-permute-done | bytes 8224 | tf_op jit(solution)/shard_map/ppermute | solution.py:235
  17.5 0.0 copy-start.3
  17.5 0.0 collective-permute-done.1.refs_3_
  17.5 0.0 copy-start
  17.5 3.9 %collective-permute-done.refs_2_ = bf16[2,512,128]{2,1,0:T(8,128)(2,1)S(1)} collective-permute-done((bf16[2,512,128]{2,1,0:T(8,128)(2,1)}, bf16[2,512,128]{2,1,0:T(8,128)(2,1)S(1)}, u32[]{:S(2)}, u32[]{:S(2)}) %collective-permute-start) | collective-permute-done | bytes 262176 | tf_op jit(solution)/shard_map/ppermute | solution.py:232
  21.4 0.0 copy-done.2
  21.4 0.0 copy-done.3
  21.4 0.0 copy-done
  21.4 0.0 copy-start.1
  21.4 0.7 %copy-done.1 = bf16[2,512,128]{2,1,0:T(8,128)(2,1)} copy-done((bf16[2,512,128]{2,1,0:T(8,128)(2,1)}, bf16[2,512,128]{2,1,0:T(8,128)(2,1)S(1)}, u32[]{:S(2)}) %copy-start.1) | copy-done | bytes 262168
  22.1 5.3 %render.1 = (bf16[64,32,128]{2,1,0:T(8,128)(2,1)}, f32[1,512,128]{2,1,0:T(8,128)}) custom-call(bf16[2,512,128]{2,1,0:T(8,128)(2,1)} %get-tuple-element.8.refs_0_, bf16[2,512,128]{2,1,0:T(8,128)(2,1)} %get-tuple-element.9.refs_1_, bf16[2,512,128]{2,1,0:T(8,128)(2,1)} %copy-done.1, bf16[2,512,128]{2,1,0:T(8,128)(2,1)} %copy-done, bf16[8,512]{1,0:T(8,128)(2,1)} %copy-done.2, ...), custom_call_target="tpu_custom_call" | custom-call | tf_op jit(solution)/shard_map/render/pallas_call | solution.py:175
  27.4 37.2 %all_to_all.5.part_ref = bf16[64,32,128]{2,1,0:T(8,128)(2,1)} all-to-all(bf16[64,32,128]{2,1,0:T(8,128)(2,1)} %get-tuple-element.12), channel_id=1, replica_groups=mesh['depth'=64,'tile'=4] {'depth'}, dimensions={0} | all-to-all | bytes 1048576 | tf_op jit(solution)/shard_map/all_to_all | solution.py:240
  64.7 1.8 %compose.1 = f32[4,8,128]{2,1,0:T(8,128)} custom-call(bf16[64,32,128]{2,1,0:T(8,128)(2,1)} %all_to_all.5.part_ref, s32[64]{0:T(128)} %rank_ref.1), custom_call_target="tpu_custom_call" | custom-call | tf_op jit(solution)/shard_map/compose/pallas_call | solution.py:216
Async XLA Ops:
  3.2 14.3 %collective-permute-start.1 = (bf16[2,512,128]{2,1,0:T(8,128)(2,1)}, bf16[2,512,128]{2,1,0:T(8,128)(2,1)S(1)}, u32[]{:S(2)}, u32[]{:S(2)}) collective-permute-start(bf16[2,512,128]{2,1,0:T(8,128)(2,1)} %get-tuple-element.8.refs_0_), channel_id=1, source_target_pairs={{4,0},{8,4},{12,8},{16,12},{20,16},{24,20},{28,24},{32,28},{36,32}... | collective-permute-start | bytes 786440 | tf_op jit(solution)/shard_map/ppermute | solution.py:233
  4.5 16.9 %collective-permute-start = (bf16[2,512,128]{2,1,0:T(8,128)(2,1)}, bf16[2,512,128]{2,1,0:T(8,128)(2,1)S(1)}, u32[]{:S(2)}, u32[]{:S(2)}) collective-permute-start(bf16[2,512,128]{2,1,0:T(8,128)(2,1)} %get-tuple-element.9.refs_1_), channel_id=1, source_target_pairs={{0,4},{4,8},{8,12},{12,16},{16,20},{20,24},{24,28},{28,32},{32,36}... | collective-permute-start | bytes 786440 | tf_op jit(solution)/shard_map/ppermute | solution.py:232
  10.3 5.6 %collective-permute-start.2 = (bf16[8,512]{1,0:T(8,128)(2,1)}, bf16[8,512]{1,0:T(8,128)(2,1)S(1)}, u32[]{:S(2)}, u32[]{:S(2)}) collective-permute-start(bf16[8,512]{1,0:T(8,128)(2,1)} %get-tuple-element.10), channel_id=1, source_target_pairs={{0,1},{1,2},{2,3},{4,5},{5,6},{6,7},{8,9},{9,10},{10,11},{12,13},{... | collective-permute-start | bytes 24584 | tf_op jit(solution)/shard_map/ppermute | solution.py:234
  12.3 5.2 %collective-permute-start.3 = (bf16[8,512]{1,0:T(8,128)(2,1)}, bf16[8,512]{1,0:T(8,128)(2,1)S(1)}, u32[]{:S(2)}, u32[]{:S(2)}) collective-permute-start(bf16[8,512]{1,0:T(8,128)(2,1)} %get-tuple-element.11), channel_id=1, source_target_pairs={{1,0},{2,1},{3,2},{5,4},{6,5},{7,6},{9,8},{10,9},{11,10},{13,12},{... | collective-permute-start | bytes 24584 | tf_op jit(solution)/shard_map/ppermute | solution.py:235
  15.9 5.5 %copy-start.2 = (bf16[8,512]{1,0:T(8,128)(2,1)}, bf16[8,512]{1,0:T(8,128)(2,1)S(1)}, u32[]{:S(2)}) copy-start(bf16[8,512]{1,0:T(8,128)(2,1)S(1)} %collective-permute-done.2.refs_4_) | copy-start | bytes 24580
  17.5 3.9 %copy-start.3 = (bf16[8,512]{1,0:T(8,128)(2,1)}, bf16[8,512]{1,0:T(8,128)(2,1)S(1)}, u32[]{:S(2)}) copy-start(bf16[8,512]{1,0:T(8,128)(2,1)S(1)} %collective-permute-done.3.refs_5_) | copy-start | bytes 24580
  17.5 3.9 %copy-start = (bf16[2,512,128]{2,1,0:T(8,128)(2,1)}, bf16[2,512,128]{2,1,0:T(8,128)(2,1)S(1)}, u32[]{:S(2)}) copy-start(bf16[2,512,128]{2,1,0:T(8,128)(2,1)S(1)} %collective-permute-done.1.refs_3_) | copy-start | bytes 786436
  21.4 0.7 %copy-start.1 = (bf16[2,512,128]{2,1,0:T(8,128)(2,1)}, bf16[2,512,128]{2,1,0:T(8,128)(2,1)S(1)}, u32[]{:S(2)}) copy-start(bf16[2,512,128]{2,1,0:T(8,128)(2,1)S(1)} %collective-permute-done.refs_2_) | copy-start | bytes 786436

commit v2 on v1

--- a/solution.py
+++ b/solution.py
@@ -14,6 +14,10 @@
 PAD = 64
 BLK = 128
 SUB = 16
+
+
+def near(x):
+    return pltpu.with_memory_space_constraint(x, pltpu.VMEM)
 
 
 def dot(a, b, dims=NN):
@@ -67,8 +71,8 @@
 
 def refine(residual, coarse, levels):
     dep, rows, cols = residual.shape
-    plane = jax.ShapeDtypeStruct((dep // 2, rows, cols), BF16)
-    edge = jax.ShapeDtypeStruct((2 * dep, rows), BF16)
+    plane = pltpu.VMEM((dep // 2, rows, cols), BF16)
+    edge = pltpu.VMEM((2 * dep, rows), BF16)
     return pl.pallas_call(
         refine_kernel,
         out_shape=(plane, plane, edge, edge),
@@ -175,7 +179,7 @@
     return pl.pallas_call(
         lambda *refs: render_kernel(step, *refs),
         out_shape=(
-            jax.ShapeDtypeStruct((rows // 8, 32, cols), BF16),
+            pltpu.VMEM((rows // 8, 32, cols), BF16),
             jax.ShapeDtypeStruct((1, rows, cols), F32),
         ),
         in_specs=[VMEM] * 6 + [SMEM] * 4,
@@ -186,7 +190,7 @@
             pltpu.VMEM((2, BLK, 2 * cols), F32),
         ],
         name="render",
-    )(low, high, before, after, left, right, rank, angles, slope, shift)
+    )(*(near(x) for x in (low, high, before, after, left, right)), rank, angles, slope, shift)
 
 
 def compose_kernel(part_ref, rank_ref, image_ref):
@@ -219,7 +223,7 @@
         in_specs=[VMEM, SMEM],
         out_specs=VMEM,
         name="compose",
-    )(parts, rank)
+    )(near(parts), rank)
 
 
 def shards(coarse, residual, levels, slab_rank, light_angles, color_slope, color_shift):

time: 66.8 us -> 63.8 us (0.955)
  Pallas kernels: 9.71 us -> 7.99 us
  local copies, waits for them, and re-layouts: 0.72 us -> 0 us
    unnamed x8 -> x0, local copies, waits for them, and re-layouts: 0.72 us -> none
    pallas_call x1, Pallas kernels: 5.3 us -> 4.59 us  [render(): pl.pallas_call(lambda *refs: render_kernel(step, *refs), out_shape=(pltpu...]
where the time goes in v2:
time: 63.8 us; the launch traced here: 63.5 us
  blocking collectives  37 us (58%)
  starting transfers between devices  12.7 us (20%)
  Pallas kernels  7.99 us (13%)
  waiting for transfers between devices  5.15 us (8%)
  between operations  0.67 us (1%)
    all_to_all x1, blocking collectives, shards(): lax.all_to_all(image, 'depth', split_axis=0, concat_axis=0, tiled=True)  37 us
    ppermute x1, starting transfers between devices, shards(): before = lax.ppermute(high, 'depth', fore(slabs))  5.82 us
    pallas_call x1, Pallas kernels, render(): pl.pallas_call(lambda *refs: render_kernel(step, *refs), out_shape=(pltpu...  4.59 us
    ppermute x1, waiting for transfers between devices, shards(): before = lax.ppermute(high, 'depth', fore(slabs))  3.81 us
    ppermute x1, starting transfers between devices, shards(): right = lax.ppermute(down, 'tile', back(tiles))  3.64 us
    pallas_call x1, Pallas kernels, refine(): pl.pallas_call(refine_kernel, out_shape=(plane, plane, edge, edge), in_sp...  1.97 us
    ppermute x1, starting transfers between devices, shards(): left = lax.ppermute(up, 'tile', fore(tiles))  1.92 us
    pallas_call x1, Pallas kernels, compose(): pl.pallas_call(compose_kernel, out_shape=jax.ShapeDtypeStruct((4, 8, part...  1.43 us
  transfers between devices with their start and end apart: 4, of which 2 were waited for; matrix products, arithmetic and copies ran while one was open for 0% of the time, Pallas kernels for 0%

profile of v2, /device:TPU:32, one launch (start us, length us, event | category | flops | bytes accessed | tf_op | source)
XLA Modules:
  0.0 63.5 jit_solution(7042658268587780791)
XLA Ops:
  0.6 2.0 %refine.1 = (bf16[2,512,128]{2,1,0:T(8,128)(2,1)S(1)}, bf16[2,512,128]{2,1,0:T(8,128)(2,1)S(1)}, bf16[8,512]{1,0:T(8,128)(2,1)S(1)}, bf16[8,512]{1,0:T(8,128)(2,1)S(1)}) custom-call(bf16[4,512,128]{2,1,0:T(8,128)(2,1)} %res_ref.1, bf16[2,64,256]{2,1,0:T(8,128)(2,1)} %bitcast.4, s32[32,128]{1,0:T(8,128)} %bitcast.5), custom_call_target="tpu_custom_call" | custom-call | tf_op jit(solution)/shard_map/refine/pallas_call | solution.py:76
  2.6 1.3 %collective-permute-start.1 = (bf16[2,512,128]{2,1,0:T(8,128)(2,1)S(1)}, bf16[2,512,128]{2,1,0:T(8,128)(2,1)S(1)}, u32[]{:S(2)}, u32[]{:S(2)}) collective-permute-start(bf16[2,512,128]{2,1,0:T(8,128)(2,1)S(1)} %get-tuple-element.8.refs_0_), channel_id=1, source_target_pairs={{4,0},{8,4},{12,8},{16,12},{20,16},{24,20},{28,24},{32,28},{36,32}... | collective-permute-start | bytes 786440 | tf_op jit(solution)/shard_map/ppermute | solution.py:237
  3.9 5.8 %collective-permute-start = (bf16[2,512,128]{2,1,0:T(8,128)(2,1)S(1)}, bf16[2,512,128]{2,1,0:T(8,128)(2,1)S(1)}, u32[]{:S(2)}, u32[]{:S(2)}) collective-permute-start(bf16[2,512,128]{2,1,0:T(8,128)(2,1)S(1)} %get-tuple-element.9.refs_1_), channel_id=1, source_target_pairs={{0,4},{4,8},{8,12},{12,16},{16,20},{20,24},{24,28},{28,32},{32,36}... | collective-permute-start | bytes 786440 | tf_op jit(solution)/shard_map/ppermute | solution.py:236
  9.7 1.9 %collective-permute-start.2 = (bf16[8,512]{1,0:T(8,128)(2,1)S(1)}, bf16[8,512]{1,0:T(8,128)(2,1)S(1)}, u32[]{:S(2)}, u32[]{:S(2)}) collective-permute-start(bf16[8,512]{1,0:T(8,128)(2,1)S(1)} %get-tuple-element.10), channel_id=1, source_target_pairs={{0,1},{1,2},{2,3},{4,5},{5,6},{6,7},{8,9},{9,10},{10,11},{12,13},{... | collective-permute-start | bytes 24584 | tf_op jit(solution)/shard_map/ppermute | solution.py:238
  11.7 3.6 %collective-permute-start.3 = (bf16[8,512]{1,0:T(8,128)(2,1)S(1)}, bf16[8,512]{1,0:T(8,128)(2,1)S(1)}, u32[]{:S(2)}, u32[]{:S(2)}) collective-permute-start(bf16[8,512]{1,0:T(8,128)(2,1)S(1)} %get-tuple-element.11), channel_id=1, source_target_pairs={{1,0},{2,1},{3,2},{5,4},{6,5},{7,6},{9,8},{10,9},{11,10},{13,12},{... | collective-permute-start | bytes 24584 | tf_op jit(solution)/shard_map/ppermute | solution.py:239
  15.3 0.0 collective-permute-done.2.refs_4_
  15.3 1.3 %collective-permute-done.3.refs_5_ = bf16[8,512]{1,0:T(8,128)(2,1)S(1)} collective-permute-done((bf16[8,512]{1,0:T(8,128)(2,1)S(1)}, bf16[8,512]{1,0:T(8,128)(2,1)S(1)}, u32[]{:S(2)}, u32[]{:S(2)}) %collective-permute-start.3) | collective-permute-done | bytes 8224 | tf_op jit(solution)/shard_map/ppermute | solution.py:239
  16.7 0.0 collective-permute-done.1.refs_3_
  16.7 3.8 %collective-permute-done.refs_2_ = bf16[2,512,128]{2,1,0:T(8,128)(2,1)S(1)} collective-permute-done((bf16[2,512,128]{2,1,0:T(8,128)(2,1)S(1)}, bf16[2,512,128]{2,1,0:T(8,128)(2,1)S(1)}, u32[]{:S(2)}, u32[]{:S(2)}) %collective-permute-start) | collective-permute-done | bytes 262176 | tf_op jit(solution)/shard_map/ppermute | solution.py:236
  20.5 4.6 %render.1 = (bf16[64,32,128]{2,1,0:T(8,128)(2,1)S(1)}, f32[1,512,128]{2,1,0:T(8,128)}) custom-call(bf16[2,512,128]{2,1,0:T(8,128)(2,1)S(1)} %get-tuple-element.8.refs_0_, bf16[2,512,128]{2,1,0:T(8,128)(2,1)S(1)} %get-tuple-element.9.refs_1_, bf16[2,512,128]{2,1,0:T(8,128)(2,1)S(1)} %collective-permute-done.refs_2_, ...), custom_call_target="tpu_custom_call" | custom-call | tf_op jit(solution)/shard_map/render/pallas_call | solution.py:179
  25.1 37.0 %all_to_all.5.part_ref = bf16[64,32,128]{2,1,0:T(8,128)(2,1)S(1)} all-to-all(bf16[64,32,128]{2,1,0:T(8,128)(2,1)S(1)} %get-tuple-element.12), channel_id=1, replica_groups=mesh['depth'=64,'tile'=4] {'depth'}, dimensions={0} | all-to-all | bytes 1048576 | tf_op jit(solution)/shard_map/all_to_all | solution.py:244
  62.1 1.4 %compose.1 = f32[4,8,128]{2,1,0:T(8,128)} custom-call(bf16[64,32,128]{2,1,0:T(8,128)(2,1)S(1)} %all_to_all.5.part_ref, s32[64]{0:T(128)} %rank_ref.1), custom_call_target="tpu_custom_call" | custom-call | tf_op jit(solution)/shard_map/compose/pallas_call | solution.py:220
Async XLA Ops:
  2.6 14.1 %collective-permute-start.1 = (bf16[2,512,128]{2,1,0:T(8,128)(2,1)S(1)}, bf16[2,512,128]{2,1,0:T(8,128)(2,1)S(1)}, u32[]{:S(2)}, u32[]{:S(2)}) collective-permute-start(bf16[2,512,128]{2,1,0:T(8,128)(2,1)S(1)} %get-tuple-element.8.refs_0_), channel_id=1, source_target_pairs={{4,0},{8,4},{12,8},{16,12},{20,16},{24,20},{28,24},{32,28},{36,32}... | collective-permute-start | bytes 786440 | tf_op jit(solution)/shard_map/ppermute | solution.py:237
  3.9 16.6 %collective-permute-start = (bf16[2,512,128]{2,1,0:T(8,128)(2,1)S(1)}, bf16[2,512,128]{2,1,0:T(8,128)(2,1)S(1)}, u32[]{:S(2)}, u32[]{:S(2)}) collective-permute-start(bf16[2,512,128]{2,1,0:T(8,128)(2,1)S(1)} %get-tuple-element.9.refs_1_), channel_id=1, source_target_pairs={{0,4},{4,8},{8,12},{12,16},{16,20},{20,24},{24,28},{28,32},{32,36}... | collective-permute-start | bytes 786440 | tf_op jit(solution)/shard_map/ppermute | solution.py:236
  9.7 5.6 %collective-permute-start.2 = (bf16[8,512]{1,0:T(8,128)(2,1)S(1)}, bf16[8,512]{1,0:T(8,128)(2,1)S(1)}, u32[]{:S(2)}, u32[]{:S(2)}) collective-permute-start(bf16[8,512]{1,0:T(8,128)(2,1)S(1)} %get-tuple-element.10), channel_id=1, source_target_pairs={{0,1},{1,2},{2,3},{4,5},{5,6},{6,7},{8,9},{9,10},{10,11},{12,13},{... | collective-permute-start | bytes 24584 | tf_op jit(solution)/shard_map/ppermute | solution.py:238
  11.7 5.0 %collective-permute-start.3 = (bf16[8,512]{1,0:T(8,128)(2,1)S(1)}, bf16[8,512]{1,0:T(8,128)(2,1)S(1)}, u32[]{:S(2)}, u32[]{:S(2)}) collective-permute-start(bf16[8,512]{1,0:T(8,128)(2,1)S(1)} %get-tuple-element.11), channel_id=1, source_target_pairs={{1,0},{2,1},{3,2},{5,4},{6,5},{7,6},{9,8},{10,9},{11,10},{13,12},{... | collective-permute-start | bytes 24584 | tf_op jit(solution)/shard_map/ppermute | solution.py:239

commit v3 on v2

v3 whole, which is shorter than its diff:
```python
import jax
import jax.numpy as jnp
from jax import lax
from jax.experimental import pallas as pl
from jax.experimental.pallas import tpu as pltpu
from jax.sharding import PartitionSpec as P

F32 = jnp.float32
BF16 = jnp.bfloat16
VMEM = pl.BlockSpec(memory_space=pltpu.VMEM)
SMEM = pl.BlockSpec(memory_space=pltpu.SMEM)
NN = (((1,), (0,)), ((), ()))
NT = (((1,), (1,)), ((), ()))
PAD = 64
BLK = 128
SUB = 16


GRANT = pltpu.CompilerParams(vmem_limit_bytes=12 * 2**20)
GAIN = 16.0


def far(x):
    return pltpu.with_memory_space_constraint(x, pltpu.HBM)


def near(x):
    return pltpu.with_memory_space_constraint(x, pltpu.VMEM)


def dot(a, b, dims=NN):
    return lax.dot_general(a, b, dims, preferred_element_type=F32)


def iota2(shape):
    return (
        lax.broadcasted_iota(jnp.int32, shape, 0),
        lax.broadcasted_iota(jnp.int32, shape, 1),
    )


def repeater(out, inner):
    r, c = iota2((out, inner))
    return jnp.where(r // (out // inner) == c, 1.0, 0.0).astype(BF16)


def stencil(offset):
    w = jnp.where(offset == -2, 1.0, jnp.where(offset == -1, -8.0, 0.0))
    return jnp.where(offset == 1, 8.0, jnp.where(offset == 2, -1.0, w))


def encode(x):
    x = x * GAIN
    x = x * x
    return x * x


def decode(x):
    for _ in range(2):
        x = x * lax.rsqrt(jnp.maximum(x, 1e-37))
    return x * (1.0 / GAIN)


def refine_kernel(
    res_ref, coarse_ref, level_ref, full_ref, z1_ref, z2_ref, x1_ref, x2_ref
):
    dep, rows, cols = res_ref.shape
    half = coarse_ref.shape[2]
    even_z = lax.rem(lax.axis_index("depth"), 2) == 0
    even_x = lax.rem(lax.axis_index("tile"), 2) == 0
    widen2 = repeater(cols, coarse_ref.shape[1])
    widen4 = repeater(cols, level_ref.shape[0])
    lev = dot(widen4, level_ref[...].astype(F32).astype(BF16)).astype(BF16)
    scale = 0.5 * dot(repeater(rows, lev.shape[1]), lev, NT)
    tall2 = repeater(256, 128)
    k, c = iota2((16, cols))
    edges = jnp.zeros((16, rows), F32)
    for zc in range(dep // 2):
        wide = dot(widen2, coarse_ref[zc]).astype(BF16)
        lifted = [dot(tall2, wide[:, b * 128 : (b + 1) * 128], NT) for b in range(half // 128)]
        for z in (2 * zc, 2 * zc + 1):
            for b in range(half // 128):
                part = pl.ds(b * 256, 256)
                full_ref[z, part, :] = (
                    lifted[b] + scale[b * 256 : (b + 1) * 256] * res_ref[z, part, :].astype(F32)
                ).astype(BF16)
            col = jnp.where(k < 8, k - 2 * z + cols - 2, k - 8 - 2 * z)
            mine = (k % 8) // 2 == z
            pick = jnp.where(mine & (col == c), 1.0, 0.0).astype(BF16)
            edges = edges + dot(pick, full_ref[z], NT)
    for p in range(2):
        z1_ref[p] = jnp.where(even_z, full_ref[2 + p], full_ref[p])
        z2_ref[p] = jnp.where(even_z, full_ref[p], full_ref[2 + p])
    last, first = edges[0:8], edges[8:16]
    x1_ref[...] = jnp.where(even_x, last, first).astype(BF16)
    x2_ref[...] = jnp.where(even_x, first, last).astype(BF16)


def refine(residual, coarse, levels):
    dep, rows, cols = residual.shape
    plane = pltpu.VMEM((2, rows, cols), BF16)
    edge = pltpu.VMEM((2 * dep, rows), BF16)
    return pl.pallas_call(
        refine_kernel,
        out_shape=(pltpu.VMEM((dep, rows, cols), BF16), plane, plane, edge, edge),
        in_specs=[VMEM] * 3,
        out_specs=(VMEM,) * 5,
        cost_estimate=pl.CostEstimate(flops=10**8, bytes_accessed=10**6, transcendentals=0),
        compiler_params=GRANT,
        name="refine",
    )(*(far(x) for x in (residual, jnp.swapaxes(coarse, 1, 2), jnp.swapaxes(levels[0], 0, 1))))


def prepare_kernel(
    step, full_ref, x1_ref, x2_ref, rank_ref, angle_ref, slope_ref, shift_ref,
    lit_ref, size_ref, coef_ref, cover_ref, flag_ref, pair, gx_ref, gy_ref,
):
    dep, rows, cols = full_ref.shape
    slabs = rank_ref.shape[0]
    even_x = lax.rem(lax.axis_index("tile"), 2) == 0
    ascending = rank_ref[0] < rank_ref[slabs - 1]
    visible = jnp.where(rank_ref[lax.axis_index("depth")] >= 0, 1.0, 0.0).astype(F32)
    azimuth = jnp.full((SUB, cols), angle_ref[0], F32)
    elevation = jnp.full((SUB, cols), angle_ref[1], F32)
    light_y = jnp.cos(elevation) * jnp.sin(azimuth)
    light_x = jnp.cos(elevation) * jnp.cos(azimuth)
    slope = [0.5 * slope_ref[k] for k in range(3)]
    shift = [0.5 * shift_ref[k] for k in range(3)]
    flag_ref[0] = jnp.sin(elevation)
    flag_ref[1] = jnp.full((SUB, cols), jnp.where(ascending, 1.0, 0.0), F32)

    zero = jnp.zeros((PAD, 2 * cols), BF16)
    for p in range(2):
        pair[p, 0:PAD, :] = zero
        pair[p, PAD + rows :, :] = zero
        for q in range(2):
            pair[p, PAD : PAD + rows, q * cols : (q + 1) * cols] = full_ref[2 * p + q]

    r, c = iota2((cols, cols))
    across = stencil(r - c).astype(BF16)
    r, c = iota2((BLK, BLK + 2 * PAD))
    along = stencil(c - PAD - r).astype(BF16)
    k, c = iota2((16, cols))
    spot = jnp.where(k < 8, k % 2 - 2, cols + k % 2)
    beside = [
        jnp.where((k % 8) // 2 == z, stencil(spot - c), 0.0).astype(BF16) for z in range(4)
    ]
    x1, x2 = x1_ref[...].astype(F32), x2_ref[...].astype(F32)
    columns = jnp.concatenate([jnp.where(even_x, x2, x1), jnp.where(even_x, x1, x2)], 0)
    columns = columns.T.astype(BF16)

    for b in range(rows // BLK):
        base = b * BLK
        for p in range(2):
            gy_ref[p] = dot(along, pair[p, base : base + BLK + 2 * PAD, :])
            for q in range(2):
                z = 2 * p + q
                gx_ref[z] = dot(full_ref[z, base : base + BLK, :], across) + dot(
                    columns[base : base + BLK], beside[z]
                )

        def some_rows(i, carry, base=base):
            at = pl.ds(pl.multiple_of(i * SUB, SUB), SUB)
            row = pl.ds(pl.multiple_of(base + i * SUB, SUB), SUB)
            clear, color = [], []
            for z in range(4):
                v = full_ref[z, row, :].astype(F32)
                gy = gy_ref[z // 2, at, (z % 2) * cols : (z % 2 + 1) * cols]
                gx = gx_ref[z, at, :]
                lit_ref[z, row, :] = light_y * gy + light_x * gx
                size_ref[z, row, :] = gy * gy + gx * gx + 144.0
                extinct = 2.0 + 2.0 * jnp.tanh(1.5 * v - 2.25)
                clear.append(jnp.exp(-step * extinct))
                color.append([0.5 + 0.5 * jnp.tanh(slope[n] * v + shift[n]) for n in range(3)])
            up = [None, clear[0], clear[0] * clear[1], None]
            up[3] = up[2] * clear[2]
            down = [None, None, clear[3], None]
            down[1] = clear[3] * clear[2]
            down[0] = down[1] * clear[1]
            before = [
                jnp.where(ascending, 1.0, down[0]),
                jnp.where(ascending, up[1], down[1]),
                jnp.where(ascending, up[2], down[2]),
                jnp.where(ascending, up[3], 1.0),
            ]
            for z in range(4):
                weight = before[z] * (1.0 - clear[z]) * visible
                for n in range(3):
                    coef_ref[3 * z + n, row, :] = weight * color[z][n]
            cover_ref[row, :] = encode((1.0 - up[3] * clear[3]) * visible)
            return carry

        lax.fori_loop(0, BLK // SUB, some_rows, 0, unroll=2)


def prepare(step, full, x1, x2, rank, angles, slope, shift):
    dep, rows, cols = full.shape
    plane = lambda n: pltpu.VMEM((n, rows, cols), F32)
    return pl.pallas_call(
        lambda *refs: prepare_kernel(step, *refs),
        out_shape=(
            plane(dep), plane(dep), plane(3 * dep), pltpu.VMEM((rows, cols), F32),
            pltpu.VMEM((2, SUB, cols), F32),
        ),
        in_specs=[VMEM] * 3 + [SMEM] * 4,
        out_specs=(VMEM,) * 5,
        scratch_shapes=[
            pltpu.VMEM((2, rows + 2 * PAD, 2 * cols), BF16),
            pltpu.VMEM((4, BLK, cols), F32),
            pltpu.VMEM((2, BLK, 2 * cols), F32),
        ],
        cost_estimate=pl.CostEstimate(flops=10**9, bytes_accessed=10**6, transcendentals=0),
        compiler_params=GRANT,
        name="prepare",
    )(*(near(x) for x in (full, x1, x2)), *(far(x) for x in (rank, angles, slope, shift)))


def shade_kernel(
    full_ref, z1_ref, z2_ref, lit_ref, size_ref, coef_ref, cover_ref, flag_ref,
    image_ref, shade_ref,
):
    _, rows, cols = full_ref.shape
    even_z = lax.rem(lax.axis_index("depth"), 2) == 0
    light_z = flag_ref[0]

    def some_rows(i, carry):
        row = pl.ds(pl.multiple_of(i * SUB, SUB), SUB)
        own = [full_ref[z, row, :].astype(F32) for z in range(4)]
        one = [z1_ref[q, row, :].astype(F32) for q in range(2)]
        two = [z2_ref[q, row, :].astype(F32) for q in range(2)]
        planes = (
            [jnp.where(even_z, two[q], one[q]) for q in range(2)]
            + own
            + [jnp.where(even_z, one[q], two[q]) for q in range(2)]
        )
        shade = []
        for z in range(4):
            gz = (planes[z] - planes[z + 4]) + 8.0 * (planes[z + 3] - planes[z + 1])
            lit = lit_ref[z, row, :] + light_z * gz
            size = size_ref[z, row, :] + gz * gz
            shade.append(0.25 + 0.75 * (jnp.abs(lit) * lax.rsqrt(size)))
        out = []
        for n in range(3):
            part = [shade[z] * coef_ref[3 * z + n, row, :] for z in range(4)]
            out.append(encode((part[0] + part[1]) + (part[2] + part[3])))
        out.append(cover_ref[row, :])
        for half in range(SUB // 8):
            tile = jnp.concatenate([x[half * 8 : half * 8 + 8] for x in out], 0)
            image_ref[i * (SUB // 8) + half] = tile.astype(image_ref.dtype)
        shade_ref[0, row, :] = 0.25 * ((shade[0] + shade[1]) + (shade[2] + shade[3]))
        return carry

    lax.fori_loop(0, rows // SUB, some_rows, 0, unroll=4)


def shade(full, z1, z2, lit, size, coef, cover, flag):
    _, rows, cols = full.shape
    return pl.pallas_call(
        shade_kernel,
        out_shape=(
            pltpu.VMEM((rows // 8, 32, cols), BF16),
            jax.ShapeDtypeStruct((1, rows, cols), F32),
        ),
        in_specs=[VMEM] * 8,
        out_specs=(VMEM, VMEM),
        compiler_params=GRANT,
        name="shade",
    )(*(near(x) for x in (full, z1, z2, lit, size, coef, cover, flag)))


def compose_kernel(part_ref, flag_ref, image_ref):
    slabs, _, cols = part_ref.shape
    ascending = jnp.max(flag_ref[1, 0:8, :]) > 0.5

    def body(i, carry):
        through, red, green, blue = carry
        tile = decode(part_ref[jnp.where(ascending, i, slabs - 1 - i)].astype(F32))
        red = red + through * tile[0:8]
        green = green + through * tile[8:16]
        blue = blue + through * tile[16:24]
        return (through * (1.0 - tile[24:32]), red, green, blue)

    zero = jnp.zeros((8, cols), F32)
    through, red, green, blue = lax.fori_loop(
        0, slabs, body, (jnp.ones((8, cols), F32), zero, zero, zero), unroll=8
    )
    image_ref[0] = red
    image_ref[1] = green
    image_ref[2] = blue
    image_ref[3] = 1.0 - through


def compose(parts, flag):
    return pl.pallas_call(
        compose_kernel,
        out_shape=jax.ShapeDtypeStruct((4, 8, parts.shape[2]), F32),
        in_specs=[VMEM, VMEM],
        out_specs=VMEM,
        compiler_params=GRANT,
        name="compose",
    )(near(parts), near(flag))


def mates(count, start):
    low = range(start, count - 1, 2)
    return [(i, i + 1) for i in low] + [(i + 1, i) for i in low]


def shards(coarse, residual, levels, slab_rank, light_angles, color_slope, color_shift):
    dep = residual.shape[0]
    slabs, tiles = lax.axis_size("depth"), lax.axis_size("tile")
    step = 4.0 / (dep * slabs)
    full, z1, z2, x1, x2 = refine(residual, coarse, levels)
    z1 = lax.ppermute(z1, "depth", mates(slabs, 0))
    z2 = lax.ppermute(z2, "depth", mates(slabs, 1))
    x1 = lax.ppermute(x1, "tile", mates(tiles, 0))
    x2 = lax.ppermute(x2, "tile", mates(tiles, 1))
    ready = prepare(step, full, x1, x2, slab_rank, light_angles, color_slope, color_shift)
    image, mean = shade(full, z1, z2, *ready)
    parts = lax.all_to_all(image, "depth", split_axis=0, concat_axis=0, tiled=True)
    return (compose(parts, ready[-1]), mean)


def solution(mesh):
    placed = (
        P("depth", None, "tile"),
        P("depth", None, "tile"),
        P("depth", None, "tile"),
        P(),
        P(),
        P(),
        P(),
    )
    return jax.shard_map(
        shards,
        mesh=mesh,
        in_specs=placed,
        out_specs=(P(None, "depth", "tile"), P("depth", None, "tile")),
        check_vma=False,
    )
```

time: 63.8 us -> 59.2 us (0.928)
  the two profiles are of different devices: /device:TPU:32 before, /device:TPU:1 now
where the time goes in v3:
time: 59.2 us; the launch traced here: 59 us
  blocking collectives  38.7 us (65%)
  starting transfers between devices  8.99 us (15%)
  Pallas kernels  8.19 us (14%)
  waiting for transfers between devices  2.52 us (4%)
  between operations  0.67 us (1%)
    all_to_all x1, blocking collectives, shards(): lax.all_to_all(image, 'depth', split_axis=0, concat_axis=0, tiled=True)  38.7 us
    ppermute x1, starting transfers between devices, shards(): z1 = lax.ppermute(z1, 'depth', mates(slabs, 0))  3.83 us
    ppermute x1, starting transfers between devices, shards(): x2 = lax.ppermute(x2, 'tile', mates(tiles, 1))  3.45 us
    pallas_call x1, Pallas kernels, prepare(): pl.pallas_call(lambda *refs: prepare_kernel(step, *refs), out_shape=(plan...  3.33 us
    pallas_call x1, Pallas kernels, refine(): pl.pallas_call(refine_kernel, out_shape=(pltpu.VMEM((dep, rows, cols), BF...  2.04 us
    pallas_call x1, Pallas kernels, shade(): pl.pallas_call(shade_kernel, out_shape=(pltpu.VMEM((rows // 8, 32, cols),...  1.67 us
    ppermute x1, waiting for transfers between devices, shards(): x2 = lax.ppermute(x2, 'tile', mates(tiles, 1))  1.49 us
  transfers between devices with their start and end apart: 4, of which 2 were waited for; matrix products, arithmetic and copies ran while one was open for 0% of the time, Pallas kernels for 6%

profile of v3, /device:TPU:1, one launch (start us, length us, event | category | flops | bytes accessed | tf_op | source)
XLA Modules:
  0.0 59.0 jit_solution(16996574297469277498)
XLA Ops:
  0.6 2.0 %refine.1 = (bf16[4,512,128]{2,1,0:T(8,128)(2,1)S(1)}, bf16[2,512,128]{2,1,0:T(8,128)(2,1)S(1)}, bf16[2,512,128]{2,1,0:T(8,128)(2,1)S(1)}, bf16[8,512]{1,0:T(8,128)(2,1)S(1)}, bf16[8,512]{1,0:T(8,128)(2,1)S(1)}) custom-call(bf16[4,512,128]{2,1,0:T(8,128)(2,1)} %res_ref.1, bf16[2,64,256]{2,1,0:T(8,128)(2,1)} %bitcast.4, s32[32,128]{1,0:T(8,128)} %bitcast.5), custom_call_target="tpu_custom_call" | custom-call | flops 100000000 | bytes 1000000 | tf_op jit(solution)/shard_map/refine/pallas_call | solution.py:103
  2.7 3.8 %collective-permute-start = (bf16[2,512,128]{2,1,0:T(8,128)(2,1)S(1)}, bf16[2,512,128]{2,1,0:T(8,128)(2,1)S(1)}, u32[]{:S(2)}, u32[]{:S(2)}) collective-permute-start(bf16[2,512,128]{2,1,0:T(8,128)(2,1)S(1)} %get-tuple-element.15), channel_id=1, source_target_pairs={{0,4},{8,12},{16,20},{24,28},{32,36},{40,44},{48,52},{56,60},{64,6... | collective-permute-start | bytes 786440 | tf_op jit(solution)/shard_map/ppermute | solution.py:314
  6.5 0.7 %collective-permute-start.1 = (bf16[2,512,128]{2,1,0:T(8,128)(2,1)S(1)}, bf16[2,512,128]{2,1,0:T(8,128)(2,1)S(1)}, u32[]{:S(2)}, u32[]{:S(2)}) collective-permute-start(bf16[2,512,128]{2,1,0:T(8,128)(2,1)S(1)} %get-tuple-element.16), channel_id=1, source_target_pairs={{4,8},{12,16},{20,24},{28,32},{36,40},{44,48},{52,56},{60,64},{68,... | collective-permute-start | bytes 786440 | tf_op jit(solution)/shard_map/ppermute | solution.py:315
  7.2 1.0 %collective-permute-start.2 = (bf16[8,512]{1,0:T(8,128)(2,1)S(1)}, bf16[8,512]{1,0:T(8,128)(2,1)S(1)}, u32[]{:S(2)}, u32[]{:S(2)}) collective-permute-start(bf16[8,512]{1,0:T(8,128)(2,1)S(1)} %get-tuple-element.17), channel_id=1, source_target_pairs={{0,1},{2,3},{1,0},{3,2},{4,5},{6,7},{5,4},{7,6},{8,9},{10,11},{9,8... | collective-permute-start | bytes 24584 | tf_op jit(solution)/shard_map/ppermute | solution.py:316
  8.2 3.4 %collective-permute-start.3 = (bf16[8,512]{1,0:T(8,128)(2,1)S(1)}, bf16[8,512]{1,0:T(8,128)(2,1)S(1)}, u32[]{:S(2)}, u32[]{:S(2)}) collective-permute-start(bf16[8,512]{1,0:T(8,128)(2,1)S(1)} %get-tuple-element.18), channel_id=1, source_target_pairs={{1,2},{2,1},{5,6},{6,5},{9,10},{10,9},{13,14},{14,13},{17,18},{18,... | collective-permute-start | bytes 24584 | tf_op jit(solution)/shard_map/ppermute | solution.py:317
  11.7 0.0 collective-permute-done.2.refs_1_
  11.7 1.5 %collective-permute-done.3.refs_2_ = bf16[8,512]{1,0:T(8,128)(2,1)S(1)} collective-permute-done((bf16[8,512]{1,0:T(8,128)(2,1)S(1)}, bf16[8,512]{1,0:T(8,128)(2,1)S(1)}, u32[]{:S(2)}, u32[]{:S(2)}) %collective-permute-start.3) | collective-permute-done | bytes 8224 | tf_op jit(solution)/shard_map/ppermute | solution.py:317
  13.2 3.3 %prepare.1 = (f32[4,512,128]{2,1,0:T(8,128)S(1)}, f32[4,512,128]{2,1,0:T(8,128)S(1)}, f32[12,512,128]{2,1,0:T(8,128)S(1)}, f32[512,128]{1,0:T(8,128)S(1)}, f32[2,16,128]{2,1,0:T(8,128)S(1)}) custom-call(bf16[4,512,128]{2,1,0:T(8,128)(2,1)S(1)} %get-tuple-element.14.refs_0_.full_ref, bf16[8,512]{1,0:T(8,128)(2,1)S(1)} %collective-permute-done.2.refs_1_, ...), custom_call_target="tpu_custom_call" | custom-call | flops 1000000000 | bytes 1000000 | tf_op jit(solution)/shard_map/prepare/pallas_call | solution.py:199
  16.5 1.0 %collective-permute-done.z1_ref = bf16[2,512,128]{2,1,0:T(8,128)(2,1)S(1)} collective-permute-done((bf16[2,512,128]{2,1,0:T(8,128)(2,1)S(1)}, bf16[2,512,128]{2,1,0:T(8,128)(2,1)S(1)}, u32[]{:S(2)}, u32[]{:S(2)}) %collective-permute-start) | collective-permute-done | bytes 262176 | tf_op jit(solution)/shard_map/ppermute | solution.py:314
  17.5 0.0 collective-permute-done.1.z2_ref
  17.5 1.7 %shade.1 = (bf16[64,32,128]{2,1,0:T(8,128)(2,1)S(1)}, f32[1,512,128]{2,1,0:T(8,128)}) custom-call(bf16[4,512,128]{2,1,0:T(8,128)(2,1)S(1)} %get-tuple-element.14.refs_0_.full_ref, bf16[2,512,128]{2,1,0:T(8,128)(2,1)S(1)} %collective-permute-done.z1_ref, bf16[2,512,128]{2,1,0:T(8,128)(2,1)S(1)} %collective-permute-done.1.z2_ref, ...), custom_call_target="tpu_custom_call" | custom-call | tf_op jit(solution)/shard_map/shade/pallas_call | solution.py:258
  19.2 38.7 %all_to_all.5.part_ref = bf16[64,32,128]{2,1,0:T(8,128)(2,1)S(1)} all-to-all(bf16[64,32,128]{2,1,0:T(8,128)(2,1)S(1)} %get-tuple-element.24), channel_id=1, replica_groups=mesh['depth'=64,'tile'=4] {'depth'}, dimensions={0} | all-to-all | bytes 1048576 | tf_op jit(solution)/shard_map/all_to_all | solution.py:320
  57.9 1.1 %compose.1 = f32[4,8,128]{2,1,0:T(8,128)} custom-call(bf16[64,32,128]{2,1,0:T(8,128)(2,1)S(1)} %all_to_all.5.part_ref, f32[2,16,128]{2,1,0:T(8,128)S(1)} %get-tuple-element.23.flag_ref), custom_call_target="tpu_custom_call" | custom-call | tf_op jit(solution)/shard_map/compose/pallas_call | solution.py:294
Async XLA Ops:
  2.7 14.9 %collective-permute-start = (bf16[2,512,128]{2,1,0:T(8,128)(2,1)S(1)}, bf16[2,512,128]{2,1,0:T(8,128)(2,1)S(1)}, u32[]{:S(2)}, u32[]{:S(2)}) collective-permute-start(bf16[2,512,128]{2,1,0:T(8,128)(2,1)S(1)} %get-tuple-element.15), channel_id=1, source_target_pairs={{0,4},{8,12},{16,20},{24,28},{32,36},{40,44},{48,52},{56,60},{64,6... | collective-permute-start | bytes 786440 | tf_op jit(solution)/shard_map/ppermute | solution.py:314
  6.5 11.0 %collective-permute-start.1 = (bf16[2,512,128]{2,1,0:T(8,128)(2,1)S(1)}, bf16[2,512,128]{2,1,0:T(8,128)(2,1)S(1)}, u32[]{:S(2)}, u32[]{:S(2)}) collective-permute-start(bf16[2,512,128]{2,1,0:T(8,128)(2,1)S(1)} %get-tuple-element.16), channel_id=1, source_target_pairs={{4,8},{12,16},{20,24},{28,32},{36,40},{44,48},{52,56},{60,64},{68,... | collective-permute-start | bytes 786440 | tf_op jit(solution)/shard_map/ppermute | solution.py:315
  7.2 4.5 %collective-permute-start.2 = (bf16[8,512]{1,0:T(8,128)(2,1)S(1)}, bf16[8,512]{1,0:T(8,128)(2,1)S(1)}, u32[]{:S(2)}, u32[]{:S(2)}) collective-permute-start(bf16[8,512]{1,0:T(8,128)(2,1)S(1)} %get-tuple-element.17), channel_id=1, source_target_pairs={{0,1},{2,3},{1,0},{3,2},{4,5},{6,7},{5,4},{7,6},{8,9},{10,11},{9,8... | collective-permute-start | bytes 24584 | tf_op jit(solution)/shard_map/ppermute | solution.py:316
  8.2 5.0 %collective-permute-start.3 = (bf16[8,512]{1,0:T(8,128)(2,1)S(1)}, bf16[8,512]{1,0:T(8,128)(2,1)S(1)}, u32[]{:S(2)}, u32[]{:S(2)}) collective-permute-start(bf16[8,512]{1,0:T(8,128)(2,1)S(1)} %get-tuple-element.18), channel_id=1, source_target_pairs={{1,2},{2,1},{5,6},{6,5},{9,10},{10,9},{13,14},{14,13},{17,18},{18,... | collective-permute-start | bytes 24584 | tf_op jit(solution)/shard_map/ppermute | solution.py:317

commit v4 on v3

--- a/solution.py
+++ b/solution.py
@@ -311,10 +311,10 @@
     slabs, tiles = lax.axis_size("depth"), lax.axis_size("tile")
     step = 4.0 / (dep * slabs)
     full, z1, z2, x1, x2 = refine(residual, coarse, levels)
+    x2 = lax.ppermute(x2, "tile", mates(tiles, 1))
     z1 = lax.ppermute(z1, "depth", mates(slabs, 0))
     z2 = lax.ppermute(z2, "depth", mates(slabs, 1))
     x1 = lax.ppermute(x1, "tile", mates(tiles, 0))
-    x2 = lax.ppermute(x2, "tile", mates(tiles, 1))
     ready = prepare(step, full, x1, x2, slab_rank, light_angles, color_slope, color_shift)
     image, mean = shade(full, z1, z2, *ready)
     parts = lax.all_to_all(image, "depth", split_axis=0, concat_axis=0, tiled=True)

time: 59.2 us -> 59.2 us (level)
  no operation moved by 1% of the time
where the time goes in v4:
time: 59.2 us; the launch traced here: 59 us
  blocking collectives  38.7 us (65%)
  starting transfers between devices  8.99 us (15%)
  Pallas kernels  8.19 us (14%)
  waiting for transfers between devices  2.52 us (4%)
  between operations  0.67 us (1%)
    all_to_all x1, blocking collectives, shards(): lax.all_to_all(image, 'depth', split_axis=0, concat_axis=0, tiled=True)  38.7 us
    ppermute x1, starting transfers between devices, shards(): z1 = lax.ppermute(z1, 'depth', mates(slabs, 0))  3.83 us
    ppermute x1, starting transfers between devices, shards(): x2 = lax.ppermute(x2, 'tile', mates(tiles, 1))  3.45 us
    pallas_call x1, Pallas kernels, prepare(): pl.pallas_call(lambda *refs: prepare_kernel(step, *refs), out_shape=(plan...  3.33 us
    pallas_call x1, Pallas kernels, refine(): pl.pallas_call(refine_kernel, out_shape=(pltpu.VMEM((dep, rows, cols), BF...  2.04 us
    pallas_call x1, Pallas kernels, shade(): pl.pallas_call(shade_kernel, out_shape=(pltpu.VMEM((rows // 8, 32, cols),...  1.67 us
    ppermute x1, waiting for transfers between devices, shards(): x2 = lax.ppermute(x2, 'tile', mates(tiles, 1))  1.49 us
  transfers between devices with their start and end apart: 4, of which 2 were waited for; matrix products, arithmetic and copies ran while one was open for 0% of the time, Pallas kernels for 6%

profile of v4, /device:TPU:1, one launch (start us, length us, event | category | flops | bytes accessed | tf_op | source)
XLA Modules:
  0.0 59.0 jit_solution(16996574297469277498)
XLA Ops:
  0.6 2.0 %refine.1 = (bf16[4,512,128]{2,1,0:T(8,128)(2,1)S(1)}, bf16[2,512,128]{2,1,0:T(8,128)(2,1)S(1)}, bf16[2,512,128]{2,1,0:T(8,128)(2,1)S(1)}, bf16[8,512]{1,0:T(8,128)(2,1)S(1)}, bf16[8,512]{1,0:T(8,128)(2,1)S(1)}) custom-call(bf16[4,512,128]{2,1,0:T(8,128)(2,1)} %res_ref.1, bf16[2,64,256]{2,1,0:T(8,128)(2,1)} %bitcast.4, s32[32,128]{1,0:T(8,128)} %bitcast.5), custom_call_target="tpu_custom_call" | custom-call | flops 100000000 | bytes 1000000 | tf_op jit(solution)/shard_map/refine/pallas_call | solution.py:103
  2.7 3.8 %collective-permute-start = (bf16[2,512,128]{2,1,0:T(8,128)(2,1)S(1)}, bf16[2,512,128]{2,1,0:T(8,128)(2,1)S(1)}, u32[]{:S(2)}, u32[]{:S(2)}) collective-permute-start(bf16[2,512,128]{2,1,0:T(8,128)(2,1)S(1)} %get-tuple-element.15), channel_id=1, source_target_pairs={{0,4},{8,12},{16,20},{24,28},{32,36},{40,44},{48,52},{56,60},{64,6... | collective-permute-start | bytes 786440 | tf_op jit(solution)/shard_map/ppermute | solution.py:315
  6.5 0.7 %collective-permute-start.1 = (bf16[2,512,128]{2,1,0:T(8,128)(2,1)S(1)}, bf16[2,512,128]{2,1,0:T(8,128)(2,1)S(1)}, u32[]{:S(2)}, u32[]{:S(2)}) collective-permute-start(bf16[2,512,128]{2,1,0:T(8,128)(2,1)S(1)} %get-tuple-element.16), channel_id=1, source_target_pairs={{4,8},{12,16},{20,24},{28,32},{36,40},{44,48},{52,56},{60,64},{68,... | collective-permute-start | bytes 786440 | tf_op jit(solution)/shard_map/ppermute | solution.py:316
  7.2 1.0 %collective-permute-start.2 = (bf16[8,512]{1,0:T(8,128)(2,1)S(1)}, bf16[8,512]{1,0:T(8,128)(2,1)S(1)}, u32[]{:S(2)}, u32[]{:S(2)}) collective-permute-start(bf16[8,512]{1,0:T(8,128)(2,1)S(1)} %get-tuple-element.17), channel_id=1, source_target_pairs={{0,1},{2,3},{1,0},{3,2},{4,5},{6,7},{5,4},{7,6},{8,9},{10,11},{9,8... | collective-permute-start | bytes 24584 | tf_op jit(solution)/shard_map/ppermute | solution.py:317
  8.2 3.4 %collective-permute-start.3 = (bf16[8,512]{1,0:T(8,128)(2,1)S(1)}, bf16[8,512]{1,0:T(8,128)(2,1)S(1)}, u32[]{:S(2)}, u32[]{:S(2)}) collective-permute-start(bf16[8,512]{1,0:T(8,128)(2,1)S(1)} %get-tuple-element.18), channel_id=1, source_target_pairs={{1,2},{2,1},{5,6},{6,5},{9,10},{10,9},{13,14},{14,13},{17,18},{18,... | collective-permute-start | bytes 24584 | tf_op jit(solution)/shard_map/ppermute | solution.py:314
  11.7 0.0 collective-permute-done.2.refs_1_
  11.7 1.5 %collective-permute-done.3.refs_2_ = bf16[8,512]{1,0:T(8,128)(2,1)S(1)} collective-permute-done((bf16[8,512]{1,0:T(8,128)(2,1)S(1)}, bf16[8,512]{1,0:T(8,128)(2,1)S(1)}, u32[]{:S(2)}, u32[]{:S(2)}) %collective-permute-start.3) | collective-permute-done | bytes 8224 | tf_op jit(solution)/shard_map/ppermute | solution.py:314
  13.2 3.3 %prepare.1 = (f32[4,512,128]{2,1,0:T(8,128)S(1)}, f32[4,512,128]{2,1,0:T(8,128)S(1)}, f32[12,512,128]{2,1,0:T(8,128)S(1)}, f32[512,128]{1,0:T(8,128)S(1)}, f32[2,16,128]{2,1,0:T(8,128)S(1)}) custom-call(bf16[4,512,128]{2,1,0:T(8,128)(2,1)S(1)} %get-tuple-element.14.refs_0_.full_ref, bf16[8,512]{1,0:T(8,128)(2,1)S(1)} %collective-permute-done.2.refs_1_, ...), custom_call_target="tpu_custom_call" | custom-call | flops 1000000000 | bytes 1000000 | tf_op jit(solution)/shard_map/prepare/pallas_call | solution.py:199
  16.5 1.0 %collective-permute-done.z1_ref = bf16[2,512,128]{2,1,0:T(8,128)(2,1)S(1)} collective-permute-done((bf16[2,512,128]{2,1,0:T(8,128)(2,1)S(1)}, bf16[2,512,128]{2,1,0:T(8,128)(2,1)S(1)}, u32[]{:S(2)}, u32[]{:S(2)}) %collective-permute-start) | collective-permute-done | bytes 262176 | tf_op jit(solution)/shard_map/ppermute | solution.py:315
  17.5 0.0 collective-permute-done.1.z2_ref
  17.5 1.7 %shade.1 = (bf16[64,32,128]{2,1,0:T(8,128)(2,1)S(1)}, f32[1,512,128]{2,1,0:T(8,128)}) custom-call(bf16[4,512,128]{2,1,0:T(8,128)(2,1)S(1)} %get-tuple-element.14.refs_0_.full_ref, bf16[2,512,128]{2,1,0:T(8,128)(2,1)S(1)} %collective-permute-done.z1_ref, bf16[2,512,128]{2,1,0:T(8,128)(2,1)S(1)} %collective-permute-done.1.z2_ref, ...), custom_call_target="tpu_custom_call" | custom-call | tf_op jit(solution)/shard_map/shade/pallas_call | solution.py:258
  19.2 38.7 %all_to_all.5.part_ref = bf16[64,32,128]{2,1,0:T(8,128)(2,1)S(1)} all-to-all(bf16[64,32,128]{2,1,0:T(8,128)(2,1)S(1)} %get-tuple-element.24), channel_id=1, replica_groups=mesh['depth'=64,'tile'=4] {'depth'}, dimensions={0} | all-to-all | bytes 1048576 | tf_op jit(solution)/shard_map/all_to_all | solution.py:320
  57.9 1.1 %compose.1 = f32[4,8,128]{2,1,0:T(8,128)} custom-call(bf16[64,32,128]{2,1,0:T(8,128)(2,1)S(1)} %all_to_all.5.part_ref, f32[2,16,128]{2,1,0:T(8,128)S(1)} %get-tuple-element.23.flag_ref), custom_call_target="tpu_custom_call" | custom-call | tf_op jit(solution)/shard_map/compose/pallas_call | solution.py:294
Async XLA Ops:
  2.7 14.9 %collective-permute-start = (bf16[2,512,128]{2,1,0:T(8,128)(2,1)S(1)}, bf16[2,512,128]{2,1,0:T(8,128)(2,1)S(1)}, u32[]{:S(2)}, u32[]{:S(2)}) collective-permute-start(bf16[2,512,128]{2,1,0:T(8,128)(2,1)S(1)} %get-tuple-element.15), channel_id=1, source_target_pairs={{0,4},{8,12},{16,20},{24,28},{32,36},{40,44},{48,52},{56,60},{64,6... | collective-permute-start | bytes 786440 | tf_op jit(solution)/shard_map/ppermute | solution.py:315
  6.5 11.0 %collective-permute-start.1 = (bf16[2,512,128]{2,1,0:T(8,128)(2,1)S(1)}, bf16[2,512,128]{2,1,0:T(8,128)(2,1)S(1)}, u32[]{:S(2)}, u32[]{:S(2)}) collective-permute-start(bf16[2,512,128]{2,1,0:T(8,128)(2,1)S(1)} %get-tuple-element.16), channel_id=1, source_target_pairs={{4,8},{12,16},{20,24},{28,32},{36,40},{44,48},{52,56},{60,64},{68,... | collective-permute-start | bytes 786440 | tf_op jit(solution)/shard_map/ppermute | solution.py:316
  7.2 4.5 %collective-permute-start.2 = (bf16[8,512]{1,0:T(8,128)(2,1)S(1)}, bf16[8,512]{1,0:T(8,128)(2,1)S(1)}, u32[]{:S(2)}, u32[]{:S(2)}) collective-permute-start(bf16[8,512]{1,0:T(8,128)(2,1)S(1)} %get-tuple-element.17), channel_id=1, source_target_pairs={{0,1},{2,3},{1,0},{3,2},{4,5},{6,7},{5,4},{7,6},{8,9},{10,11},{9,8... | collective-permute-start | bytes 24584 | tf_op jit(solution)/shard_map/ppermute | solution.py:317
  8.2 5.0 %collective-permute-start.3 = (bf16[8,512]{1,0:T(8,128)(2,1)S(1)}, bf16[8,512]{1,0:T(8,128)(2,1)S(1)}, u32[]{:S(2)}, u32[]{:S(2)}) collective-permute-start(bf16[8,512]{1,0:T(8,128)(2,1)S(1)} %get-tuple-element.18), channel_id=1, source_target_pairs={{1,2},{2,1},{5,6},{6,5},{9,10},{10,9},{13,14},{14,13},{17,18},{18,... | collective-permute-start | bytes 24584 | tf_op jit(solution)/shard_map/ppermute | solution.py:314

commit v5 on v3

--- a/solution.py
+++ b/solution.py
@@ -1,3 +1,5 @@
+import functools
+
 import jax
 import jax.numpy as jnp
 from jax import lax
@@ -47,6 +49,11 @@
 def stencil(offset):
     w = jnp.where(offset == -2, 1.0, jnp.where(offset == -1, -8.0, 0.0))
     return jnp.where(offset == 1, 8.0, jnp.where(offset == 2, -1.0, w))
+
+
+def seat(d):
+    y, x, z = d >> 4, (d >> 2) & 3, d & 3
+    return z * 16 + (3 - y) * 4 + (3 - x)
 
 
 def encode(x):
@@ -75,22 +82,29 @@
     tall2 = repeater(256, 128)
     k, c = iota2((16, cols))
     edges = jnp.zeros((16, rows), F32)
-    for zc in range(dep // 2):
-        wide = dot(widen2, coarse_ref[zc]).astype(BF16)
-        lifted = [dot(tall2, wide[:, b * 128 : (b + 1) * 128], NT) for b in range(half // 128)]
-        for z in (2 * zc, 2 * zc + 1):
-            for b in range(half // 128):
-                part = pl.ds(b * 256, 256)
-                full_ref[z, part, :] = (
-                    lifted[b] + scale[b * 256 : (b + 1) * 256] * res_ref[z, part, :].astype(F32)
-                ).astype(BF16)
-            col = jnp.where(k < 8, k - 2 * z + cols - 2, k - 8 - 2 * z)
-            mine = (k % 8) // 2 == z
-            pick = jnp.where(mine & (col == c), 1.0, 0.0).astype(BF16)
-            edges = edges + dot(pick, full_ref[z], NT)
-    for p in range(2):
-        z1_ref[p] = jnp.where(even_z, full_ref[2 + p], full_ref[p])
-        z2_ref[p] = jnp.where(even_z, full_ref[p], full_ref[2 + p])
+    wide = [dot(widen2, coarse_ref[zc]).astype(BF16) for zc in range(dep // 2)]
+    for b in range(half // 128):
+        part = pl.ds(b * 256, 256)
+        packs = []
+        for zc in range(dep // 2):
+            lifted = dot(tall2, wide[zc][:, b * 128 : (b + 1) * 128], NT)
+            both = [
+                lifted + scale[b * 256 : (b + 1) * 256] * res_ref[z, part, :].astype(F32)
+                for z in (2 * zc, 2 * zc + 1)
+            ]
+            for q in range(2):
+                full_ref[2 * zc + q, part, :] = both[q].astype(BF16)
+            packs.append(
+                jnp.concatenate([v.reshape(32, 8, cols) for v in both], 1).astype(BF16)
+            )
+        group = pl.ds(b * 32, 32)
+        z1_ref[group] = jnp.where(even_z, packs[1], packs[0])
+        z2_ref[group] = jnp.where(even_z, packs[0], packs[1])
+    for z in range(dep):
+        col = jnp.where(k < 8, k - 2 * z + cols - 2, k - 8 - 2 * z)
+        mine = (k % 8) // 2 == z
+        pick = jnp.where(mine & (col == c), 1.0, 0.0).astype(BF16)
+        edges = edges + dot(pick, full_ref[z], NT)
     last, first = edges[0:8], edges[8:16]
     x1_ref[...] = jnp.where(even_x, last, first).astype(BF16)
     x2_ref[...] = jnp.where(even_x, first, last).astype(BF16)
@@ -98,7 +112,7 @@
 
 def refine(residual, coarse, levels):
     dep, rows, cols = residual.shape
-    plane = pltpu.VMEM((2, rows, cols), BF16)
+    plane = pltpu.VMEM((rows // 8, 16, cols), BF16)
     edge = pltpu.VMEM((2 * dep, rows), BF16)
     return pl.pallas_call(
         refine_kernel,
@@ -113,7 +127,7 @@
 
 def prepare_kernel(
     step, full_ref, x1_ref, x2_ref, rank_ref, angle_ref, slope_ref, shift_ref,
-    lit_ref, size_ref, coef_ref, cover_ref, flag_ref, pair, gx_ref, gy_ref,
+    lit_ref, size_ref, part_ref, coef_ref, cover_ref, flag_ref, pair, gx_ref, gy_ref,
 ):
     dep, rows, cols = full_ref.shape
     slabs = rank_ref.shape[0]
@@ -162,9 +176,14 @@
         def some_rows(i, carry, base=base):
             at = pl.ds(pl.multiple_of(i * SUB, SUB), SUB)
             row = pl.ds(pl.multiple_of(base + i * SUB, SUB), SUB)
+            own = [full_ref[z, row, :].astype(F32) for z in range(4)]
+            part_ref[0, row, :] = 8.0 * own[1] - own[2]
+            part_ref[1, row, :] = 8.0 * (own[2] - own[0]) - own[3]
+            part_ref[2, row, :] = 8.0 * (own[3] - own[1]) + own[0]
+            part_ref[3, row, :] = own[1] - 8.0 * own[2]
             clear, color = [], []
             for z in range(4):
-                v = full_ref[z, row, :].astype(F32)
+                v = own[z]
                 gy = gy_ref[z // 2, at, (z % 2) * cols : (z % 2 + 1) * cols]
                 gx = gx_ref[z, at, :]
                 lit_ref[z, row, :] = light_y * gy + light_x * gx
@@ -199,11 +218,11 @@
     return pl.pallas_call(
         lambda *refs: prepare_kernel(step, *refs),
         out_shape=(
-            plane(dep), plane(dep), plane(3 * dep), pltpu.VMEM((rows, cols), F32),
+            plane(dep), plane(dep), plane(dep), plane(3 * dep), pltpu.VMEM((rows, cols), F32),
             pltpu.VMEM((2, SUB, cols), F32),
         ),
         in_specs=[VMEM] * 3 + [SMEM] * 4,
-        out_specs=(VMEM,) * 5,
+        out_specs=(VMEM,) * 6,
         scratch_shapes=[
             pltpu.VMEM((2, rows + 2 * PAD, 2 * cols), BF16),
             pltpu.VMEM((4, BLK, cols), F32),
@@ -216,45 +235,49 @@
 
 
 def shade_kernel(
-    full_ref, z1_ref, z2_ref, lit_ref, size_ref, coef_ref, cover_ref, flag_ref,
-    image_ref, shade_ref,
+    z1_ref, z2_ref, lit_ref, size_ref, part_ref, coef_ref, cover_ref, flag_ref,
+    image_ref, mean_ref,
 ):
-    _, rows, cols = full_ref.shape
+    cols = lit_ref.shape[2]
     even_z = lax.rem(lax.axis_index("depth"), 2) == 0
-    light_z = flag_ref[0]
-
-    def some_rows(i, carry):
-        row = pl.ds(pl.multiple_of(i * SUB, SUB), SUB)
-        own = [full_ref[z, row, :].astype(F32) for z in range(4)]
-        one = [z1_ref[q, row, :].astype(F32) for q in range(2)]
-        two = [z2_ref[q, row, :].astype(F32) for q in range(2)]
-        planes = (
-            [jnp.where(even_z, two[q], one[q]) for q in range(2)]
-            + own
-            + [jnp.where(even_z, one[q], two[q]) for q in range(2)]
+    light_z = flag_ref[0, 0:8, :]
+
+    def group(i, carry, start=0, z1_ref=z1_ref):
+        r = start + i
+        row = pl.ds(pl.multiple_of(8 * r, 8), 8)
+        one, two = z1_ref[i].astype(F32), z2_ref[r].astype(F32)
+        low = jnp.where(even_z, two, one)
+        high = jnp.where(even_z, one, two)
+        part = [part_ref[z, row, :] for z in range(4)]
+        gz = (
+            part[0] + (low[0:8] - 8.0 * low[8:16]),
+            part[1] + low[8:16],
+            part[2] - high[0:8],
+            part[3] + (8.0 * high[0:8] - high[8:16]),
         )
         shade = []
         for z in range(4):
-            gz = (planes[z] - planes[z + 4]) + 8.0 * (planes[z + 3] - planes[z + 1])
-            lit = lit_ref[z, row, :] + light_z * gz
-            size = size_ref[z, row, :] + gz * gz
+            lit = lit_ref[z, row, :] + light_z * gz[z]
+            size = size_ref[z, row, :] + gz[z] * gz[z]
             shade.append(0.25 + 0.75 * (jnp.abs(lit) * lax.rsqrt(size)))
         out = []
         for n in range(3):
-            part = [shade[z] * coef_ref[3 * z + n, row, :] for z in range(4)]
-            out.append(encode((part[0] + part[1]) + (part[2] + part[3])))
+            p = [shade[z] * coef_ref[3 * z + n, row, :] for z in range(4)]
+            out.append(encode((p[0] + p[1]) + (p[2] + p[3])))
         out.append(cover_ref[row, :])
-        for half in range(SUB // 8):
-            tile = jnp.concatenate([x[half * 8 : half * 8 + 8] for x in out], 0)
-            image_ref[i * (SUB // 8) + half] = tile.astype(image_ref.dtype)
-        shade_ref[0, row, :] = 0.25 * ((shade[0] + shade[1]) + (shade[2] + shade[3]))
+        image_ref[seat(r)] = jnp.concatenate(out, 0).astype(BF16)
+        mean_ref[0, row, :] = 0.25 * ((shade[0] + shade[1]) + (shade[2] + shade[3]))
         return carry
 
-    lax.fori_loop(0, rows // SUB, some_rows, 0, unroll=4)
-
-
-def shade(full, z1, z2, lit, size, coef, cover, flag):
-    _, rows, cols = full.shape
+    start = 0
+    for ref in (z1_ref,):
+        body = functools.partial(group, start=start, z1_ref=ref)
+        lax.fori_loop(0, ref.shape[0], body, 0, unroll=8)
+        start += ref.shape[0]
+
+
+def shade(z1, z2, ready):
+    _, rows, cols = ready[0].shape
     return pl.pallas_call(
         shade_kernel,
         out_shape=(
@@ -265,7 +288,7 @@
         out_specs=(VMEM, VMEM),
         compiler_params=GRANT,
         name="shade",
-    )(*(near(x) for x in (full, z1, z2, lit, size, coef, cover, flag)))
+    )(*(near(x) for x in (z1, z2, *ready)))
 
 
 def compose_kernel(part_ref, flag_ref, image_ref):
@@ -274,7 +297,7 @@
 
     def body(i, carry):
         through, red, green, blue = carry
-        tile = decode(part_ref[jnp.where(ascending, i, slabs - 1 - i)].astype(F32))
+        tile = decode(part_ref[seat(jnp.where(ascending, i, slabs - 1 - i))].astype(F32))
         red = red + through * tile[0:8]
         green = green + through * tile[8:16]
         blue = blue + through * tile[16:24]
@@ -316,8 +339,11 @@
     x1 = lax.ppermute(x1, "tile", mates(tiles, 0))
     x2 = lax.ppermute(x2, "tile", mates(tiles, 1))
     ready = prepare(step, full, x1, x2, slab_rank, light_angles, color_slope, color_shift)
-    image, mean = shade(full, z1, z2, *ready)
-    parts = lax.all_to_all(image, "depth", split_axis=0, concat_axis=0, tiled=True)
+    image, mean = shade(z1, z2, ready)
+    order = sorted(range(slabs), key=seat)
+    parts = lax.all_to_all(
+        image, "depth", split_axis=0, concat_axis=0, tiled=True, axis_index_groups=[order]
+    )
     return (compose(parts, ready[-1]), mean)
 
 

time: 59.2 us -> 55.8 us (0.943)
  blocking collectives: 38.7 us -> 35.6 us
    all_to_all x1, blocking collectives: 38.7 us -> 35.6 us  [shards(): lax.all_to_all(image, 'depth', split_axis=0, concat_axis=0, tiled=True, a...]
where the time goes in v5:
time: 55.8 us; the launch traced here: 55.6 us
  blocking collectives  35.6 us (64%)
  starting transfers between devices  9.01 us (16%)
  Pallas kernels  7.91 us (14%)
  waiting for transfers between devices  2.45 us (4%)
  between operations  0.66 us (1%)
    all_to_all x1, blocking collectives, shards(): lax.all_to_all(image, 'depth', split_axis=0, concat_axis=0, tiled=True, a...  35.6 us
    ppermute x1, starting transfers between devices, shards(): z1 = lax.ppermute(z1, 'depth', mates(slabs, 0))  3.86 us
    ppermute x1, starting transfers between devices, shards(): x2 = lax.ppermute(x2, 'tile', mates(tiles, 1))  3.44 us
    pallas_call x1, Pallas kernels, prepare(): pl.pallas_call(lambda *refs: prepare_kernel(step, *refs), out_shape=(plan...  3.4 us
    pallas_call x1, Pallas kernels, refine(): pl.pallas_call(refine_kernel, out_shape=(pltpu.VMEM((dep, rows, cols), BF...  1.76 us
    pallas_call x1, Pallas kernels, shade(): pl.pallas_call(shade_kernel, out_shape=(pltpu.VMEM((rows // 8, 32, cols),...  1.53 us
    ppermute x1, waiting for transfers between devices, shards(): x2 = lax.ppermute(x2, 'tile', mates(tiles, 1))  1.5 us
    pallas_call x1, Pallas kernels, compose(): pl.pallas_call(compose_kernel, out_shape=jax.ShapeDtypeStruct((4, 8, part...  1.22 us
  transfers between devices with their start and end apart: 4, of which 2 were waited for; matrix products, arithmetic and copies ran while one was open for 0% of the time, Pallas kernels for 6%

profile of v5, /device:TPU:1, one launch (start us, length us, event | category | flops | bytes accessed | tf_op | source)
XLA Modules:
  0.0 55.6 jit_solution(3737159615554969573)
XLA Ops:
  0.6 1.8 %refine.1 = (bf16[4,512,128]{2,1,0:T(8,128)(2,1)S(1)}, bf16[64,16,128]{2,1,0:T(8,128)(2,1)S(1)}, bf16[64,16,128]{2,1,0:T(8,128)(2,1)S(1)}, bf16[8,512]{1,0:T(8,128)(2,1)S(1)}, bf16[8,512]{1,0:T(8,128)(2,1)S(1)}) custom-call(bf16[4,512,128]{2,1,0:T(8,128)(2,1)} %res_ref.1, bf16[2,64,256]{2,1,0:T(8,128)(2,1)} %bitcast.4, s32[32,128]{1,0:T(8,128)} %bitcast.5), custom_call_target="tpu_custom_call" | custom-call | flops 100000000 | bytes 1000000 | tf_op jit(solution)/shard_map/refine/pallas_call | solution.py:117
  2.4 3.9 %collective-permute-start = (bf16[64,16,128]{2,1,0:T(8,128)(2,1)S(1)}, bf16[64,16,128]{2,1,0:T(8,128)(2,1)S(1)}, u32[]{:S(2)}, u32[]{:S(2)}) collective-permute-start(bf16[64,16,128]{2,1,0:T(8,128)(2,1)S(1)} %get-tuple-element.15), channel_id=1, source_target_pairs={{0,4},{8,12},{16,20},{24,28},{32,36},{40,44},{48,52},{56,60},{64,6... | collective-permute-start | bytes 786440 | tf_op jit(solution)/shard_map/ppermute | solution.py:337
  6.3 0.7 %collective-permute-start.1 = (bf16[64,16,128]{2,1,0:T(8,128)(2,1)S(1)}, bf16[64,16,128]{2,1,0:T(8,128)(2,1)S(1)}, u32[]{:S(2)}, u32[]{:S(2)}) collective-permute-start(bf16[64,16,128]{2,1,0:T(8,128)(2,1)S(1)} %get-tuple-element.16), channel_id=1, source_target_pairs={{4,8},{12,16},{20,24},{28,32},{36,40},{44,48},{52,56},{60,64},{68,... | collective-permute-start | bytes 786440 | tf_op jit(solution)/shard_map/ppermute | solution.py:338
  6.9 1.0 %collective-permute-start.2 = (bf16[8,512]{1,0:T(8,128)(2,1)S(1)}, bf16[8,512]{1,0:T(8,128)(2,1)S(1)}, u32[]{:S(2)}, u32[]{:S(2)}) collective-permute-start(bf16[8,512]{1,0:T(8,128)(2,1)S(1)} %get-tuple-element.18), channel_id=1, source_target_pairs={{0,1},{2,3},{1,0},{3,2},{4,5},{6,7},{5,4},{7,6},{8,9},{10,11},{9,8... | collective-permute-start | bytes 24584 | tf_op jit(solution)/shard_map/ppermute | solution.py:339
  8.0 3.4 %collective-permute-start.3 = (bf16[8,512]{1,0:T(8,128)(2,1)S(1)}, bf16[8,512]{1,0:T(8,128)(2,1)S(1)}, u32[]{:S(2)}, u32[]{:S(2)}) collective-permute-start(bf16[8,512]{1,0:T(8,128)(2,1)S(1)} %get-tuple-element.19), channel_id=1, source_target_pairs={{1,2},{2,1},{5,6},{6,5},{9,10},{10,9},{13,14},{14,13},{17,18},{18,... | collective-permute-start | bytes 24584 | tf_op jit(solution)/shard_map/ppermute | solution.py:340
  11.4 0.0 collective-permute-done.2.refs_1_
  11.4 1.5 %collective-permute-done.3.refs_2_ = bf16[8,512]{1,0:T(8,128)(2,1)S(1)} collective-permute-done((bf16[8,512]{1,0:T(8,128)(2,1)S(1)}, bf16[8,512]{1,0:T(8,128)(2,1)S(1)}, u32[]{:S(2)}, u32[]{:S(2)}) %collective-permute-start.3) | collective-permute-done | bytes 8224 | tf_op jit(solution)/shard_map/ppermute | solution.py:340
  12.9 3.4 %prepare.1 = (f32[4,512,128]{2,1,0:T(8,128)S(1)}, f32[4,512,128]{2,1,0:T(8,128)S(1)}, f32[4,512,128]{2,1,0:T(8,128)S(1)}, f32[12,512,128]{2,1,0:T(8,128)S(1)}, f...) custom-call(bf16[4,512,128]{2,1,0:T(8,128)(2,1)S(1)} %get-tuple-element.17.refs_0_, ...), custom_call_target="tpu_custom_call" | custom-call | flops 1000000000 | bytes 1000000 | tf_op jit(solution)/shard_map/prepare/pallas_call | solution.py:218
  16.3 1.0 %collective-permute-done.z1_ref = bf16[64,16,128]{2,1,0:T(8,128)(2,1)S(1)} collective-permute-done((bf16[64,16,128]{2,1,0:T(8,128)(2,1)S(1)}, bf16[64,16,128]{2,1,0:T(8,128)(2,1)S(1)}, u32[]{:S(2)}, u32[]{:S(2)}) %collective-permute-start) | collective-permute-done | bytes 262176 | tf_op jit(solution)/shard_map/ppermute | solution.py:337
  17.3 0.0 collective-permute-done.1.z2_ref
  17.3 1.5 %shade.1 = (bf16[64,32,128]{2,1,0:T(8,128)(2,1)S(1)}, f32[1,512,128]{2,1,0:T(8,128)}) custom-call(bf16[64,16,128]{2,1,0:T(8,128)(2,1)S(1)} %collective-permute-done.z1_ref, bf16[64,16,128]{2,1,0:T(8,128)(2,1)S(1)} %collective-permute-done.1.z2_ref, f32[4,512,128]{2,1,0:T(8,128)S(1)} %get-tuple-element.20.lit_ref, ...), custom_call_target="tpu_custom_call" | custom-call | tf_op jit(solution)/shard_map/shade/pallas_call | solution.py:281
  18.8 35.6 %all_to_all.5.part_ref = bf16[64,32,128]{2,1,0:T(8,128)(2,1)S(1)} all-to-all(bf16[64,32,128]{2,1,0:T(8,128)(2,1)S(1)} %get-tuple-element.26), channel_id=1, replica_groups={{240,224,208,192,176,160,144,128,112,96,80,64,48,32,16,0,244,228,212,19..., dimensions={0} | all-to-all | bytes 1048576 | tf_op jit(solution)/shard_map/all_to_all | solution.py:344
  54.4 1.2 %compose.1 = f32[4,8,128]{2,1,0:T(8,128)} custom-call(bf16[64,32,128]{2,1,0:T(8,128)(2,1)S(1)} %all_to_all.5.part_ref, f32[2,16,128]{2,1,0:T(8,128)S(1)} %get-tuple-element.25.flag_ref), custom_call_target="tpu_custom_call" | custom-call | tf_op jit(solution)/shard_map/compose/pallas_call | solution.py:317
Async XLA Ops:
  2.4 14.9 %collective-permute-start = (bf16[64,16,128]{2,1,0:T(8,128)(2,1)S(1)}, bf16[64,16,128]{2,1,0:T(8,128)(2,1)S(1)}, u32[]{:S(2)}, u32[]{:S(2)}) collective-permute-start(bf16[64,16,128]{2,1,0:T(8,128)(2,1)S(1)} %get-tuple-element.15), channel_id=1, source_target_pairs={{0,4},{8,12},{16,20},{24,28},{32,36},{40,44},{48,52},{56,60},{64,6... | collective-permute-start | bytes 786440 | tf_op jit(solution)/shard_map/ppermute | solution.py:337
  6.3 11.0 %collective-permute-start.1 = (bf16[64,16,128]{2,1,0:T(8,128)(2,1)S(1)}, bf16[64,16,128]{2,1,0:T(8,128)(2,1)S(1)}, u32[]{:S(2)}, u32[]{:S(2)}) collective-permute-start(bf16[64,16,128]{2,1,0:T(8,128)(2,1)S(1)} %get-tuple-element.16), channel_id=1, source_target_pairs={{4,8},{12,16},{20,24},{28,32},{36,40},{44,48},{52,56},{60,64},{68,... | collective-permute-start | bytes 786440 | tf_op jit(solution)/shard_map/ppermute | solution.py:338
  6.9 4.5 %collective-permute-start.2 = (bf16[8,512]{1,0:T(8,128)(2,1)S(1)}, bf16[8,512]{1,0:T(8,128)(2,1)S(1)}, u32[]{:S(2)}, u32[]{:S(2)}) collective-permute-start(bf16[8,512]{1,0:T(8,128)(2,1)S(1)} %get-tuple-element.18), channel_id=1, source_target_pairs={{0,1},{2,3},{1,0},{3,2},{4,5},{6,7},{5,4},{7,6},{8,9},{10,11},{9,8... | collective-permute-start | bytes 24584 | tf_op jit(solution)/shard_map/ppermute | solution.py:339
  8.0 5.0 %collective-permute-start.3 = (bf16[8,512]{1,0:T(8,128)(2,1)S(1)}, bf16[8,512]{1,0:T(8,128)(2,1)S(1)}, u32[]{:S(2)}, u32[]{:S(2)}) collective-permute-start(bf16[8,512]{1,0:T(8,128)(2,1)S(1)} %get-tuple-element.19), channel_id=1, source_target_pairs={{1,2},{2,1},{5,6},{6,5},{9,10},{10,9},{13,14},{14,13},{17,18},{18,... | collective-permute-start | bytes 24584 | tf_op jit(solution)/shard_map/ppermute | solution.py:340

commit v6 on v5

--- a/solution.py
+++ b/solution.py
@@ -73,7 +73,7 @@
 ):
     dep, rows, cols = res_ref.shape
     half = coarse_ref.shape[2]
-    even_z = lax.rem(lax.axis_index("depth"), 2) == 0
+    even_z = lax.rem(lax.axis_index("depth"), 2) == 1
     even_x = lax.rem(lax.axis_index("tile"), 2) == 0
     widen2 = repeater(cols, coarse_ref.shape[1])
     widen4 = repeater(cols, level_ref.shape[0])
@@ -126,12 +126,11 @@
 
 
 def prepare_kernel(
-    step, full_ref, x1_ref, x2_ref, rank_ref, angle_ref, slope_ref, shift_ref,
-    lit_ref, size_ref, part_ref, coef_ref, cover_ref, flag_ref, pair, gx_ref, gy_ref,
+    step, full_ref, rank_ref, angle_ref, slope_ref, shift_ref,
+    lit_ref, size_ref, part_ref, coef_ref, cover_ref, flag_ref, gx_ref, pair, gy_ref,
 ):
     dep, rows, cols = full_ref.shape
     slabs = rank_ref.shape[0]
-    even_x = lax.rem(lax.axis_index("tile"), 2) == 0
     ascending = rank_ref[0] < rank_ref[slabs - 1]
     visible = jnp.where(rank_ref[lax.axis_index("depth")] >= 0, 1.0, 0.0).astype(F32)
     azimuth = jnp.full((SUB, cols), angle_ref[0], F32)
@@ -142,6 +141,7 @@
     shift = [0.5 * shift_ref[k] for k in range(3)]
     flag_ref[0] = jnp.sin(elevation)
     flag_ref[1] = jnp.full((SUB, cols), jnp.where(ascending, 1.0, 0.0), F32)
+    flag_ref[2] = light_x
 
     zero = jnp.zeros((PAD, 2 * cols), BF16)
     for p in range(2):
@@ -154,24 +154,13 @@
     across = stencil(r - c).astype(BF16)
     r, c = iota2((BLK, BLK + 2 * PAD))
     along = stencil(c - PAD - r).astype(BF16)
-    k, c = iota2((16, cols))
-    spot = jnp.where(k < 8, k % 2 - 2, cols + k % 2)
-    beside = [
-        jnp.where((k % 8) // 2 == z, stencil(spot - c), 0.0).astype(BF16) for z in range(4)
-    ]
-    x1, x2 = x1_ref[...].astype(F32), x2_ref[...].astype(F32)
-    columns = jnp.concatenate([jnp.where(even_x, x2, x1), jnp.where(even_x, x1, x2)], 0)
-    columns = columns.T.astype(BF16)
-
     for b in range(rows // BLK):
         base = b * BLK
         for p in range(2):
             gy_ref[p] = dot(along, pair[p, base : base + BLK + 2 * PAD, :])
             for q in range(2):
                 z = 2 * p + q
-                gx_ref[z] = dot(full_ref[z, base : base + BLK, :], across) + dot(
-                    columns[base : base + BLK], beside[z]
-                )
+                gx_ref[z, base : base + BLK, :] = dot(full_ref[z, base : base + BLK, :], across)
 
         def some_rows(i, carry, base=base):
             at = pl.ds(pl.multiple_of(i * SUB, SUB), SUB)
@@ -185,7 +174,7 @@
             for z in range(4):
                 v = own[z]
                 gy = gy_ref[z // 2, at, (z % 2) * cols : (z % 2 + 1) * cols]
-                gx = gx_ref[z, at, :]
+                gx = gx_ref[z, row, :]
                 lit_ref[z, row, :] = light_y * gy + light_x * gx
                 size_ref[z, row, :] = gy * gy + gx * gx + 144.0
                 extinct = 2.0 + 2.0 * jnp.tanh(1.5 * v - 2.25)
@@ -212,26 +201,56 @@
         lax.fori_loop(0, BLK // SUB, some_rows, 0, unroll=2)
 
 
-def prepare(step, full, x1, x2, rank, angles, slope, shift):
+def prepare(step, full, rank, angles, slope, shift):
     dep, rows, cols = full.shape
     plane = lambda n: pltpu.VMEM((n, rows, cols), F32)
     return pl.pallas_call(
         lambda *refs: prepare_kernel(step, *refs),
         out_shape=(
             plane(dep), plane(dep), plane(dep), plane(3 * dep), pltpu.VMEM((rows, cols), F32),
-            pltpu.VMEM((2, SUB, cols), F32),
+            pltpu.VMEM((3, SUB, cols), F32), plane(dep),
         ),
-        in_specs=[VMEM] * 3 + [SMEM] * 4,
-        out_specs=(VMEM,) * 6,
+        in_specs=[VMEM] + [SMEM] * 4,
+        out_specs=(VMEM,) * 7,
         scratch_shapes=[
             pltpu.VMEM((2, rows + 2 * PAD, 2 * cols), BF16),
-            pltpu.VMEM((4, BLK, cols), F32),
             pltpu.VMEM((2, BLK, 2 * cols), F32),
         ],
         cost_estimate=pl.CostEstimate(flops=10**9, bytes_accessed=10**6, transcendentals=0),
         compiler_params=GRANT,
         name="prepare",
-    )(*(near(x) for x in (full, x1, x2)), *(far(x) for x in (rank, angles, slope, shift)))
+    )(near(full), *(far(x) for x in (rank, angles, slope, shift)))
+
+
+def mend_kernel(lit_ref, size_ref, gx_ref, flag_ref, x1_ref, x2_ref, lit_out, size_out):
+    dep, rows, cols = lit_ref.shape
+    even_x = lax.rem(lax.axis_index("tile"), 2) == 0
+    k, c = iota2((16, cols))
+    spot = jnp.where(k < 8, k % 2 - 2, cols + k % 2)
+    x1, x2 = x1_ref[...].astype(F32), x2_ref[...].astype(F32)
+    columns = jnp.concatenate([jnp.where(even_x, x2, x1), jnp.where(even_x, x1, x2)], 0)
+    columns = columns.T.astype(BF16)
+    light_x = flag_ref[2, 0:1, :]
+    for z in range(dep):
+        beside = jnp.where((k % 8) // 2 == z, stencil(spot - c), 0.0).astype(BF16)
+        for b in range(rows // BLK):
+            row = slice(b * BLK, (b + 1) * BLK)
+            more = dot(columns[row], beside)
+            lit_out[z, row, :] = lit_ref[z, row, :] + light_x * more
+            size_out[z, row, :] = size_ref[z, row, :] + more * (2.0 * gx_ref[z, row, :] + more)
+
+
+def mend(lit, size, gx, flag, x1, x2):
+    return pl.pallas_call(
+        mend_kernel,
+        out_shape=(pltpu.VMEM(lit.shape, F32), pltpu.VMEM(size.shape, F32)),
+        in_specs=[VMEM] * 6,
+        out_specs=(VMEM, VMEM),
+        input_output_aliases={0: 0, 1: 1},
+        cost_estimate=pl.CostEstimate(flops=10**8, bytes_accessed=10**6, transcendentals=0),
+        compiler_params=GRANT,
+        name="mend",
+    )(*(near(x) for x in (lit, size, gx, flag, x1, x2)))
 
 
 def shade_kernel(
@@ -239,7 +258,7 @@
     image_ref, mean_ref,
 ):
     cols = lit_ref.shape[2]
-    even_z = lax.rem(lax.axis_index("depth"), 2) == 0
+    even_z = lax.rem(lax.axis_index("depth"), 2) == 1
     light_z = flag_ref[0, 0:8, :]
 
     def group(i, carry, start=0, z1_ref=z1_ref):
@@ -282,7 +301,7 @@
         shade_kernel,
         out_shape=(
             pltpu.VMEM((rows // 8, 32, cols), BF16),
-            jax.ShapeDtypeStruct((1, rows, cols), F32),
+            pltpu.VMEM((1, rows, cols), F32),
         ),
         in_specs=[VMEM] * 8,
         out_specs=(VMEM, VMEM),
@@ -291,7 +310,9 @@
     )(*(near(x) for x in (z1, z2, *ready)))
 
 
-def compose_kernel(part_ref, flag_ref, image_ref):
+def compose_kernel(part_ref, flag_ref, mean_ref, image_ref, out_ref, sem):
+    copy = pltpu.make_async_copy(mean_ref, out_ref, sem)
+    copy.start()
     slabs, _, cols = part_ref.shape
     ascending = jnp.max(flag_ref[1, 0:8, :]) > 0.5
 
@@ -311,17 +332,22 @@
     image_ref[1] = green
     image_ref[2] = blue
     image_ref[3] = 1.0 - through
-
-
-def compose(parts, flag):
+    copy.wait()
+
+
+def compose(parts, flag, mean):
     return pl.pallas_call(
         compose_kernel,
-        out_shape=jax.ShapeDtypeStruct((4, 8, parts.shape[2]), F32),
-        in_specs=[VMEM, VMEM],
-        out_specs=VMEM,
+        out_shape=(
+            jax.ShapeDtypeStruct((4, 8, parts.shape[2]), F32),
+            jax.ShapeDtypeStruct(mean.shape, F32),
+        ),
+        in_specs=[VMEM] * 3,
+        out_specs=(VMEM, pl.BlockSpec(memory_space=pltpu.HBM)),
+        scratch_shapes=[pltpu.SemaphoreType.DMA],
         compiler_params=GRANT,
         name="compose",
-    )(near(parts), near(flag))
+    )(near(parts), near(flag), near(mean))
 
 
 def mates(count, start):
@@ -334,17 +360,18 @@
     slabs, tiles = lax.axis_size("depth"), lax.axis_size("tile")
     step = 4.0 / (dep * slabs)
     full, z1, z2, x1, x2 = refine(residual, coarse, levels)
-    z1 = lax.ppermute(z1, "depth", mates(slabs, 0))
-    z2 = lax.ppermute(z2, "depth", mates(slabs, 1))
+    z1 = lax.ppermute(z1, "depth", mates(slabs, 1))
+    z2 = lax.ppermute(z2, "depth", mates(slabs, 0))
     x1 = lax.ppermute(x1, "tile", mates(tiles, 0))
     x2 = lax.ppermute(x2, "tile", mates(tiles, 1))
-    ready = prepare(step, full, x1, x2, slab_rank, light_angles, color_slope, color_shift)
+    *ready, gx = prepare(step, full, slab_rank, light_angles, color_slope, color_shift)
+    ready[:2] = mend(*ready[:2], gx, ready[-1], x1, x2)
     image, mean = shade(z1, z2, ready)
     order = sorted(range(slabs), key=seat)
     parts = lax.all_to_all(
         image, "depth", split_axis=0, concat_axis=0, tiled=True, axis_index_groups=[order]
     )
-    return (compose(parts, ready[-1]), mean)
+    return compose(parts, ready[-1], mean)
 
 
 def solution(mesh):

time: 55.8 us -> 54 us (0.968)
  blocking collectives: 35.6 us -> 27 us
  starting transfers between devices: 9.01 us -> 13.8 us
  waiting for transfers between devices: 2.45 us -> 4.02 us
    all_to_all x1, blocking collectives: 35.6 us -> 27 us  [shards(): lax.all_to_all(image, 'depth', split_axis=0, concat_axis=0, tiled=True, a...]
    ppermute x2, starting transfers between devices: 4.52 us -> 10 us  [the longest x1 9.33 us: shards(): z2 = lax.ppermute(z2, 'depth', mates(slabs, 0))]
    ppermute x1, waiting for transfers between devices: 1.5 us -> 3.28 us  [shards(): x2 = lax.ppermute(x2, 'tile', mates(tiles, 1))]
    ppermute x1, starting transfers between devices: 3.44 us -> 2.52 us  [shards(): x2 = lax.ppermute(x2, 'tile', mates(tiles, 1))]
    pallas_call x1 -> x2, Pallas kernels: 1.22 us -> 2.12 us  [the longest x1 1.31 us: compose(): pl.pallas_call(compose_kernel, out_shape=(jax.ShapeDtypeStruct((4, 8, par...]
    pallas_call x1, Pallas kernels: 1.53 us -> 0.84 us  [shade(): pl.pallas_call(shade_kernel, out_shape=(pltpu.VMEM((rows // 8, 32, cols),...]
  transfers between devices with their start and end apart: 4 -> 4, of which waited for: 2 -> 2; matrix products, arithmetic and copies ran while one was open for 0% -> 0% of each run, Pallas kernels for 6% -> 8%
where the time goes in v6:
time: 54 us; the launch traced here: 53.5 us
  blocking collectives  27 us (50%)
  starting transfers between devices  13.8 us (26%)
  Pallas kernels  8.02 us (15%)
  waiting for transfers between devices  4.02 us (7%)
  between operations  0.68 us (1%)
    all_to_all x1, blocking collectives, shards(): lax.all_to_all(image, 'depth', split_axis=0, concat_axis=0, tiled=True, a...  27 us
    ppermute x1, starting transfers between devices, shards(): z2 = lax.ppermute(z2, 'depth', mates(slabs, 0))  9.33 us
    pallas_call x1, Pallas kernels, prepare(): pl.pallas_call(lambda *refs: prepare_kernel(step, *refs), out_shape=(plan...  3.29 us
    ppermute x1, waiting for transfers between devices, shards(): x2 = lax.ppermute(x2, 'tile', mates(tiles, 1))  3.28 us
    ppermute x1, starting transfers between devices, shards(): x2 = lax.ppermute(x2, 'tile', mates(tiles, 1))  2.52 us
    pallas_call x1, Pallas kernels, refine(): pl.pallas_call(refine_kernel, out_shape=(pltpu.VMEM((dep, rows, cols), BF...  1.76 us
    pallas_call x1, Pallas kernels, compose(): pl.pallas_call(compose_kernel, out_shape=(jax.ShapeDtypeStruct((4, 8, par...  1.31 us
    ppermute x1, starting transfers between devices, shards(): x1 = lax.ppermute(x1, 'tile', mates(tiles, 0))  1.23 us
  transfers between devices with their start and end apart: 4, of which 2 were waited for; matrix products, arithmetic and copies ran while one was open for 0% of the time, Pallas kernels for 8%

profile of v6, /device:TPU:1, one launch (start us, length us, event | category | flops | bytes accessed | tf_op | source)
XLA Modules:
  0.0 53.5 jit_solution(10789374336367737380)
XLA Ops:
  0.6 1.8 %refine.1 = (bf16[4,512,128]{2,1,0:T(8,128)(2,1)S(1)}, bf16[64,16,128]{2,1,0:T(8,128)(2,1)S(1)}, bf16[64,16,128]{2,1,0:T(8,128)(2,1)S(1)}, bf16[8,512]{1,0:T(8,128)(2,1)S(1)}, bf16[8,512]{1,0:T(8,128)(2,1)S(1)}) custom-call(bf16[4,512,128]{2,1,0:T(8,128)(2,1)} %res_ref.1, bf16[2,64,256]{2,1,0:T(8,128)(2,1)} %bitcast.4, s32[32,128]{1,0:T(8,128)} %bitcast.5), custom_call_target="tpu_custom_call" | custom-call | flops 100000000 | bytes 1000000 | tf_op jit(solution)/shard_map/refine/pallas_call | solution.py:117
  2.4 0.7 %collective-permute-start = (bf16[64,16,128]{2,1,0:T(8,128)(2,1)S(1)}, bf16[64,16,128]{2,1,0:T(8,128)(2,1)S(1)}, u32[]{:S(2)}, u32[]{:S(2)}) collective-permute-start(bf16[64,16,128]{2,1,0:T(8,128)(2,1)S(1)} %get-tuple-element.18), channel_id=1, source_target_pairs={{4,8},{12,16},{20,24},{28,32},{36,40},{44,48},{52,56},{60,64},{68,... | collective-permute-start | bytes 786440 | tf_op jit(solution)/shard_map/ppermute | solution.py:363
  3.1 9.3 %collective-permute-start.1 = (bf16[64,16,128]{2,1,0:T(8,128)(2,1)S(1)}, bf16[64,16,128]{2,1,0:T(8,128)(2,1)S(1)}, u32[]{:S(2)}, u32[]{:S(2)}) collective-permute-start(bf16[64,16,128]{2,1,0:T(8,128)(2,1)S(1)} %get-tuple-element.19), channel_id=1, source_target_pairs={{0,4},{8,12},{16,20},{24,28},{32,36},{40,44},{48,52},{56,60},{64,6... | collective-permute-start | bytes 786440 | tf_op jit(solution)/shard_map/ppermute | solution.py:364
  12.4 1.2 %collective-permute-start.2 = (bf16[8,512]{1,0:T(8,128)(2,1)S(1)}, bf16[8,512]{1,0:T(8,128)(2,1)S(1)}, u32[]{:S(2)}, u32[]{:S(2)}) collective-permute-start(bf16[8,512]{1,0:T(8,128)(2,1)S(1)} %get-tuple-element.25), channel_id=1, source_target_pairs={{0,1},{2,3},{1,0},{3,2},{4,5},{6,7},{5,4},{7,6},{8,9},{10,11},{9,8... | collective-permute-start | bytes 24584 | tf_op jit(solution)/shard_map/ppermute | solution.py:365
  13.7 2.5 %collective-permute-start.3 = (bf16[8,512]{1,0:T(8,128)(2,1)S(1)}, bf16[8,512]{1,0:T(8,128)(2,1)S(1)}, u32[]{:S(2)}, u32[]{:S(2)}) collective-permute-start(bf16[8,512]{1,0:T(8,128)(2,1)S(1)} %get-tuple-element.26), channel_id=1, source_target_pairs={{1,2},{2,1},{5,6},{6,5},{9,10},{10,9},{13,14},{14,13},{17,18},{18,... | collective-permute-start | bytes 24584 | tf_op jit(solution)/shard_map/ppermute | solution.py:366
  16.2 3.3 %prepare.1 = (f32[4,512,128]{2,1,0:T(8,128)S(1)}, f32[4,512,128]{2,1,0:T(8,128)S(1)}, f32[4,512,128]{2,1,0:T(8,128)S(1)}, f32[12,512,128]{2,1,0:T(8,128)S(1)}, f...) custom-call(bf16[4,512,128]{2,1,0:T(8,128)(2,1)S(1)} %get-tuple-element.20.refs_0_, ...), custom_call_target="tpu_custom_call" | custom-call | flops 1000000000 | bytes 1000000 | tf_op jit(solution)/shard_map/prepare/pallas_call | solution.py:207
  19.5 0.0 collective-permute-done.2.x1_ref
  19.5 3.3 %collective-permute-done.3.x2_ref = bf16[8,512]{1,0:T(8,128)(2,1)S(1)} collective-permute-done((bf16[8,512]{1,0:T(8,128)(2,1)S(1)}, bf16[8,512]{1,0:T(8,128)(2,1)S(1)}, u32[]{:S(2)}, u32[]{:S(2)}) %collective-permute-start.3) | collective-permute-done | bytes 8224 | tf_op jit(solution)/shard_map/ppermute | solution.py:366
  22.8 0.8 %mend.1 = (f32[4,512,128]{2,1,0:T(8,128)S(1)}, f32[4,512,128]{2,1,0:T(8,128)S(1)}) custom-call(f32[4,512,128]{2,1,0:T(8,128)S(1)} %get-tuple-element.21.lit_ref, f32[4,512,128]{2,1,0:T(8,128)S(1)} %get-tuple-element.22.size_ref, f32[4,512,128]{2,1,0:T(8,128)S(1)} %get-tuple-element.23.gx_ref, ...), custom_call_target="tpu_custom_call", output_to_operand_aliasing={{0}: (0, {}), {1}: (1, {})} | custom-call | flops 100000000 | bytes 1000000 | tf_op jit(solution)/shard_map/mend/pallas_call | solution.py:244
  23.6 0.0 collective-permute-done.z1_ref
  23.6 0.7 %collective-permute-done.1.z2_ref = bf16[64,16,128]{2,1,0:T(8,128)(2,1)S(1)} collective-permute-done((bf16[64,16,128]{2,1,0:T(8,128)(2,1)S(1)}, bf16[64,16,128]{2,1,0:T(8,128)(2,1)S(1)}, u32[]{:S(2)}, u32[]{:S(2)}) %collective-permute-start.1) | collective-permute-done | bytes 262176 | tf_op jit(solution)/shard_map/ppermute | solution.py:364
  24.3 0.8 %shade.1 = (bf16[64,32,128]{2,1,0:T(8,128)(2,1)S(1)}, f32[1,512,128]{2,1,0:T(8,128)S(1)}) custom-call(bf16[64,16,128]{2,1,0:T(8,128)(2,1)S(1)} %collective-permute-done.z1_ref, bf16[64,16,128]{2,1,0:T(8,128)(2,1)S(1)} %collective-permute-done.1.z2_ref, f32[4,512,128]{2,1,0:T(8,128)S(1)} %get-tuple-element.27.lit_ref, ...), custom_call_target="tpu_custom_call" | custom-call | tf_op jit(solution)/shard_map/shade/pallas_call | solution.py:300
  25.2 27.0 %all_to_all.5.part_ref = bf16[64,32,128]{2,1,0:T(8,128)(2,1)S(1)} all-to-all(bf16[64,32,128]{2,1,0:T(8,128)(2,1)S(1)} %get-tuple-element.32), channel_id=1, replica_groups={{240,224,208,192,176,160,144,128,112,96,80,64,48,32,16,0,244,228,212,19..., dimensions={0} | all-to-all | bytes 1048576 | tf_op jit(solution)/shard_map/all_to_all | solution.py:371
  52.2 1.3 %compose.1 = (f32[4,8,128]{2,1,0:T(8,128)}, f32[1,512,128]{2,1,0:T(8,128)}) custom-call(bf16[64,32,128]{2,1,0:T(8,128)(2,1)S(1)} %all_to_all.5.part_ref, f32[3,16,128]{2,1,0:T(8,128)S(1)} %get-tuple-element.24.flag_ref, f32[1,512,128]{2,1,0:T(8,128)S(1)} %get-tuple-element.33.mean_ref), custom_call_target="tpu_custom_call" | custom-call | tf_op jit(solution)/shard_map/compose/pallas_call | solution.py:339
Async XLA Ops:
  2.4 21.2 %collective-permute-start = (bf16[64,16,128]{2,1,0:T(8,128)(2,1)S(1)}, bf16[64,16,128]{2,1,0:T(8,128)(2,1)S(1)}, u32[]{:S(2)}, u32[]{:S(2)}) collective-permute-start(bf16[64,16,128]{2,1,0:T(8,128)(2,1)S(1)} %get-tuple-element.18), channel_id=1, source_target_pairs={{4,8},{12,16},{20,24},{28,32},{36,40},{44,48},{52,56},{60,64},{68,... | collective-permute-start | bytes 786440 | tf_op jit(solution)/shard_map/ppermute | solution.py:363
  3.1 21.2 %collective-permute-start.1 = (bf16[64,16,128]{2,1,0:T(8,128)(2,1)S(1)}, bf16[64,16,128]{2,1,0:T(8,128)(2,1)S(1)}, u32[]{:S(2)}, u32[]{:S(2)}) collective-permute-start(bf16[64,16,128]{2,1,0:T(8,128)(2,1)S(1)} %get-tuple-element.19), channel_id=1, source_target_pairs={{0,4},{8,12},{16,20},{24,28},{32,36},{40,44},{48,52},{56,60},{64,6... | collective-permute-start | bytes 786440 | tf_op jit(solution)/shard_map/ppermute | solution.py:364
  12.4 7.1 %collective-permute-start.2 = (bf16[8,512]{1,0:T(8,128)(2,1)S(1)}, bf16[8,512]{1,0:T(8,128)(2,1)S(1)}, u32[]{:S(2)}, u32[]{:S(2)}) collective-permute-start(bf16[8,512]{1,0:T(8,128)(2,1)S(1)} %get-tuple-element.25), channel_id=1, source_target_pairs={{0,1},{2,3},{1,0},{3,2},{4,5},{6,7},{5,4},{7,6},{8,9},{10,11},{9,8... | collective-permute-start | bytes 24584 | tf_op jit(solution)/shard_map/ppermute | solution.py:365
  13.7 9.1 %collective-permute-start.3 = (bf16[8,512]{1,0:T(8,128)(2,1)S(1)}, bf16[8,512]{1,0:T(8,128)(2,1)S(1)}, u32[]{:S(2)}, u32[]{:S(2)}) collective-permute-start(bf16[8,512]{1,0:T(8,128)(2,1)S(1)} %get-tuple-element.26), channel_id=1, source_target_pairs={{1,2},{2,1},{5,6},{6,5},{9,10},{10,9},{13,14},{14,13},{17,18},{18,... | collective-permute-start | bytes 24584 | tf_op jit(solution)/shard_map/ppermute | solution.py:366

commit v7 on v6

--- a/solution.py
+++ b/solution.py
@@ -53,7 +53,7 @@
 
 def seat(d):
     y, x, z = d >> 4, (d >> 2) & 3, d & 3
-    return z * 16 + (3 - y) * 4 + (3 - x)
+    return (3 - z) * 16 + (3 - y) * 4 + (3 - x)
 
 
 def encode(x):
@@ -69,19 +69,16 @@
 
 
 def refine_kernel(
-    res_ref, coarse_ref, level_ref, full_ref, z1_ref, z2_ref, x1_ref, x2_ref
+    res_ref, coarse_ref, level_ref, full_ref, z1_ref, z2_ref
 ):
     dep, rows, cols = res_ref.shape
     half = coarse_ref.shape[2]
     even_z = lax.rem(lax.axis_index("depth"), 2) == 1
-    even_x = lax.rem(lax.axis_index("tile"), 2) == 0
     widen2 = repeater(cols, coarse_ref.shape[1])
     widen4 = repeater(cols, level_ref.shape[0])
     lev = dot(widen4, level_ref[...].astype(F32).astype(BF16)).astype(BF16)
     scale = 0.5 * dot(repeater(rows, lev.shape[1]), lev, NT)
     tall2 = repeater(256, 128)
-    k, c = iota2((16, cols))
-    edges = jnp.zeros((16, rows), F32)
     wide = [dot(widen2, coarse_ref[zc]).astype(BF16) for zc in range(dep // 2)]
     for b in range(half // 128):
         part = pl.ds(b * 256, 256)
@@ -100,6 +97,13 @@
         group = pl.ds(b * 32, 32)
         z1_ref[group] = jnp.where(even_z, packs[1], packs[0])
         z2_ref[group] = jnp.where(even_z, packs[0], packs[1])
+
+
+def columns_kernel(full_ref, x1_ref, x2_ref):
+    dep, rows, cols = full_ref.shape
+    even_x = lax.rem(lax.axis_index("tile"), 2) == 0
+    k, c = iota2((16, cols))
+    edges = jnp.zeros((16, rows), F32)
     for z in range(dep):
         col = jnp.where(k < 8, k - 2 * z + cols - 2, k - 8 - 2 * z)
         mine = (k % 8) // 2 == z
@@ -110,15 +114,28 @@
     x2_ref[...] = jnp.where(even_x, first, last).astype(BF16)
 
 
+def columns(full):
+    dep, rows, _ = full.shape
+    edge = pltpu.VMEM((2 * dep, rows), BF16)
+    return pl.pallas_call(
+        columns_kernel,
+        out_shape=(edge, edge),
+        in_specs=[VMEM],
+        out_specs=(VMEM, VMEM),
+        cost_estimate=pl.CostEstimate(flops=10**8, bytes_accessed=10**6, transcendentals=0),
+        compiler_params=GRANT,
+        name="columns",
+    )(near(full))
+
+
 def refine(residual, coarse, levels):
     dep, rows, cols = residual.shape
     plane = pltpu.VMEM((rows // 8, 16, cols), BF16)
-    edge = pltpu.VMEM((2 * dep, rows), BF16)
     return pl.pallas_call(
         refine_kernel,
-        out_shape=(pltpu.VMEM((dep, rows, cols), BF16), plane, plane, edge, edge),
+        out_shape=(pltpu.VMEM((dep, rows, cols), BF16), plane, plane),
         in_specs=[VMEM] * 3,
-        out_specs=(VMEM,) * 5,
+        out_specs=(VMEM,) * 3,
         cost_estimate=pl.CostEstimate(flops=10**8, bytes_accessed=10**6, transcendentals=0),
         compiler_params=GRANT,
         name="refine",
@@ -359,7 +376,8 @@
     dep = residual.shape[0]
     slabs, tiles = lax.axis_size("depth"), lax.axis_size("tile")
     step = 4.0 / (dep * slabs)
-    full, z1, z2, x1, x2 = refine(residual, coarse, levels)
+    full, z1, z2 = refine(residual, coarse, levels)
+    x1, x2 = columns(full)
     z1 = lax.ppermute(z1, "depth", mates(slabs, 1))
     z2 = lax.ppermute(z2, "depth", mates(slabs, 0))
     x1 = lax.ppermute(x1, "tile", mates(tiles, 0))

time: 54 us -> 53.4 us (0.989)
  no operation moved by 1% of the time
where the time goes in v7:
time: 53.4 us; the launch traced here: 53.2 us
  blocking collectives  26.8 us (50%)
  starting transfers between devices  13.8 us (26%)
  Pallas kernels  8.1 us (15%)
  waiting for transfers between devices  3.78 us (7%)
  between operations  0.69 us (1%)
    all_to_all x1, blocking collectives, shards(): lax.all_to_all(image, 'depth', split_axis=0, concat_axis=0, tiled=True, a...  26.8 us
    ppermute x1, starting transfers between devices, shards(): z2 = lax.ppermute(z2, 'depth', mates(slabs, 0))  9.33 us
    pallas_call x1, Pallas kernels, prepare(): pl.pallas_call(lambda *refs: prepare_kernel(step, *refs), out_shape=(plan...  3.29 us
    ppermute x1, waiting for transfers between devices, shards(): x2 = lax.ppermute(x2, 'tile', mates(tiles, 1))  3.02 us
    ppermute x1, starting transfers between devices, shards(): x2 = lax.ppermute(x2, 'tile', mates(tiles, 1))  2.52 us
    pallas_call x1, Pallas kernels, refine(): pl.pallas_call(refine_kernel, out_shape=(pltpu.VMEM((dep, rows, cols), BF...  1.6 us
    pallas_call x1, Pallas kernels, compose(): pl.pallas_call(compose_kernel, out_shape=(jax.ShapeDtypeStruct((4, 8, par...  1.31 us
    ppermute x1, starting transfers between devices, shards(): x1 = lax.ppermute(x1, 'tile', mates(tiles, 0))  1.26 us
  transfers between devices with their start and end apart: 4, of which 2 were waited for; matrix products, arithmetic and copies ran while one was open for 0% of the time, Pallas kernels for 8%

profile of v7, /device:TPU:1, one launch (start us, length us, event | category | flops | bytes accessed | tf_op | source)
XLA Modules:
  0.0 53.2 jit_solution(16651239835776654780)
XLA Ops:
  0.6 1.6 %refine.1 = (bf16[4,512,128]{2,1,0:T(8,128)(2,1)S(1)}, bf16[64,16,128]{2,1,0:T(8,128)(2,1)S(1)}, bf16[64,16,128]{2,1,0:T(8,128)(2,1)S(1)}) custom-call(bf16[4,512,128]{2,1,0:T(8,128)(2,1)} %res_ref.1, bf16[2,64,256]{2,1,0:T(8,128)(2,1)} %bitcast.4, s32[32,128]{1,0:T(8,128)} %bitcast.5), custom_call_target="tpu_custom_call" | custom-call | flops 100000000 | bytes 1000000 | tf_op jit(solution)/shard_map/refine/pallas_call | solution.py:134
  2.2 0.7 %collective-permute-start = (bf16[64,16,128]{2,1,0:T(8,128)(2,1)S(1)}, bf16[64,16,128]{2,1,0:T(8,128)(2,1)S(1)}, u32[]{:S(2)}, u32[]{:S(2)}) collective-permute-start(bf16[64,16,128]{2,1,0:T(8,128)(2,1)S(1)} %get-tuple-element.18), channel_id=1, source_target_pairs={{4,8},{12,16},{20,24},{28,32},{36,40},{44,48},{52,56},{60,64},{68,... | collective-permute-start | bytes 786440 | tf_op jit(solution)/shard_map/ppermute | solution.py:381
  2.9 9.3 %collective-permute-start.1 = (bf16[64,16,128]{2,1,0:T(8,128)(2,1)S(1)}, bf16[64,16,128]{2,1,0:T(8,128)(2,1)S(1)}, u32[]{:S(2)}, u32[]{:S(2)}) collective-permute-start(bf16[64,16,128]{2,1,0:T(8,128)(2,1)S(1)} %get-tuple-element.19), channel_id=1, source_target_pairs={{0,4},{8,12},{16,20},{24,28},{32,36},{40,44},{48,52},{56,60},{64,6... | collective-permute-start | bytes 786440 | tf_op jit(solution)/shard_map/ppermute | solution.py:382
  12.2 0.2 columns.1
  12.5 1.3 %collective-permute-start.2 = (bf16[8,512]{1,0:T(8,128)(2,1)S(1)}, bf16[8,512]{1,0:T(8,128)(2,1)S(1)}, u32[]{:S(2)}, u32[]{:S(2)}) collective-permute-start(bf16[8,512]{1,0:T(8,128)(2,1)S(1)} %get-tuple-element.25), channel_id=1, source_target_pairs={{0,1},{2,3},{1,0},{3,2},{4,5},{6,7},{5,4},{7,6},{8,9},{10,11},{9,8... | collective-permute-start | bytes 24584 | tf_op jit(solution)/shard_map/ppermute | solution.py:383
  13.7 2.5 %collective-permute-start.3 = (bf16[8,512]{1,0:T(8,128)(2,1)S(1)}, bf16[8,512]{1,0:T(8,128)(2,1)S(1)}, u32[]{:S(2)}, u32[]{:S(2)}) collective-permute-start(bf16[8,512]{1,0:T(8,128)(2,1)S(1)} %get-tuple-element.26), channel_id=1, source_target_pairs={{1,2},{2,1},{5,6},{6,5},{9,10},{10,9},{13,14},{14,13},{17,18},{18,... | collective-permute-start | bytes 24584 | tf_op jit(solution)/shard_map/ppermute | solution.py:384
  16.3 3.3 %prepare.1 = (f32[4,512,128]{2,1,0:T(8,128)S(1)}, f32[4,512,128]{2,1,0:T(8,128)S(1)}, f32[4,512,128]{2,1,0:T(8,128)S(1)}, f32[12,512,128]{2,1,0:T(8,128)S(1)}, f...) custom-call(bf16[4,512,128]{2,1,0:T(8,128)(2,1)S(1)} %get-tuple-element.20.refs_0_.full_ref, ...), custom_call_target="tpu_custom_call" | custom-call | flops 1000000000 | bytes 1000000 | tf_op jit(solution)/shard_map/prepare/pallas_call | solution.py:224
  19.6 0.0 collective-permute-done.2.x1_ref
  19.6 3.0 %collective-permute-done.3.x2_ref = bf16[8,512]{1,0:T(8,128)(2,1)S(1)} collective-permute-done((bf16[8,512]{1,0:T(8,128)(2,1)S(1)}, bf16[8,512]{1,0:T(8,128)(2,1)S(1)}, u32[]{:S(2)}, u32[]{:S(2)}) %collective-permute-start.3) | collective-permute-done | bytes 8224 | tf_op jit(solution)/shard_map/ppermute | solution.py:384
  22.6 0.8 %mend.1 = (f32[4,512,128]{2,1,0:T(8,128)S(1)}, f32[4,512,128]{2,1,0:T(8,128)S(1)}) custom-call(f32[4,512,128]{2,1,0:T(8,128)S(1)} %get-tuple-element.21.lit_ref, f32[4,512,128]{2,1,0:T(8,128)S(1)} %get-tuple-element.22.size_ref, f32[4,512,128]{2,1,0:T(8,128)S(1)} %get-tuple-element.23.gx_ref, ...), custom_call_target="tpu_custom_call", output_to_operand_aliasing={{0}: (0, {}), {1}: (1, {})} | custom-call | flops 100000000 | bytes 1000000 | tf_op jit(solution)/shard_map/mend/pallas_call | solution.py:261
  23.4 0.0 collective-permute-done.z1_ref
  23.4 0.7 %collective-permute-done.1.z2_ref = bf16[64,16,128]{2,1,0:T(8,128)(2,1)S(1)} collective-permute-done((bf16[64,16,128]{2,1,0:T(8,128)(2,1)S(1)}, bf16[64,16,128]{2,1,0:T(8,128)(2,1)S(1)}, u32[]{:S(2)}, u32[]{:S(2)}) %collective-permute-start.1) | collective-permute-done | bytes 262176 | tf_op jit(solution)/shard_map/ppermute | solution.py:382
  24.2 0.9 %shade.1 = (bf16[64,32,128]{2,1,0:T(8,128)(2,1)S(1)}, f32[1,512,128]{2,1,0:T(8,128)S(1)}) custom-call(bf16[64,16,128]{2,1,0:T(8,128)(2,1)S(1)} %collective-permute-done.z1_ref, bf16[64,16,128]{2,1,0:T(8,128)(2,1)S(1)} %collective-permute-done.1.z2_ref, f32[4,512,128]{2,1,0:T(8,128)S(1)} %get-tuple-element.27.lit_ref, ...), custom_call_target="tpu_custom_call" | custom-call | tf_op jit(solution)/shard_map/shade/pallas_call | solution.py:317
  25.0 26.8 %all_to_all.5.part_ref = bf16[64,32,128]{2,1,0:T(8,128)(2,1)S(1)} all-to-all(bf16[64,32,128]{2,1,0:T(8,128)(2,1)S(1)} %get-tuple-element.32), channel_id=1, replica_groups={{252,236,220,204,188,172,156,140,124,108,92,76,60,44,28,12,248,232,216,..., dimensions={0} | all-to-all | bytes 1048576 | tf_op jit(solution)/shard_map/all_to_all | solution.py:389
  51.9 1.3 %compose.1 = (f32[4,8,128]{2,1,0:T(8,128)}, f32[1,512,128]{2,1,0:T(8,128)}) custom-call(bf16[64,32,128]{2,1,0:T(8,128)(2,1)S(1)} %all_to_all.5.part_ref, f32[3,16,128]{2,1,0:T(8,128)S(1)} %get-tuple-element.24.flag_ref, f32[1,512,128]{2,1,0:T(8,128)S(1)} %get-tuple-element.33.mean_ref), custom_call_target="tpu_custom_call" | custom-call | tf_op jit(solution)/shard_map/compose/pallas_call | solution.py:356
Async XLA Ops:
  2.2 21.2 %collective-permute-start = (bf16[64,16,128]{2,1,0:T(8,128)(2,1)S(1)}, bf16[64,16,128]{2,1,0:T(8,128)(2,1)S(1)}, u32[]{:S(2)}, u32[]{:S(2)}) collective-permute-start(bf16[64,16,128]{2,1,0:T(8,128)(2,1)S(1)} %get-tuple-element.18), channel_id=1, source_target_pairs={{4,8},{12,16},{20,24},{28,32},{36,40},{44,48},{52,56},{60,64},{68,... | collective-permute-start | bytes 786440 | tf_op jit(solution)/shard_map/ppermute | solution.py:381
  2.9 21.2 %collective-permute-start.1 = (bf16[64,16,128]{2,1,0:T(8,128)(2,1)S(1)}, bf16[64,16,128]{2,1,0:T(8,128)(2,1)S(1)}, u32[]{:S(2)}, u32[]{:S(2)}) collective-permute-start(bf16[64,16,128]{2,1,0:T(8,128)(2,1)S(1)} %get-tuple-element.19), channel_id=1, source_target_pairs={{0,4},{8,12},{16,20},{24,28},{32,36},{40,44},{48,52},{56,60},{64,6... | collective-permute-start | bytes 786440 | tf_op jit(solution)/shard_map/ppermute | solution.py:382
  12.5 7.1 %collective-permute-start.2 = (bf16[8,512]{1,0:T(8,128)(2,1)S(1)}, bf16[8,512]{1,0:T(8,128)(2,1)S(1)}, u32[]{:S(2)}, u32[]{:S(2)}) collective-permute-start(bf16[8,512]{1,0:T(8,128)(2,1)S(1)} %get-tuple-element.25), channel_id=1, source_target_pairs={{0,1},{2,3},{1,0},{3,2},{4,5},{6,7},{5,4},{7,6},{8,9},{10,11},{9,8... | collective-permute-start | bytes 24584 | tf_op jit(solution)/shard_map/ppermute | solution.py:383
  13.7 8.9 %collective-permute-start.3 = (bf16[8,512]{1,0:T(8,128)(2,1)S(1)}, bf16[8,512]{1,0:T(8,128)(2,1)S(1)}, u32[]{:S(2)}, u32[]{:S(2)}) collective-permute-start(bf16[8,512]{1,0:T(8,128)(2,1)S(1)} %get-tuple-element.26), channel_id=1, source_target_pairs={{1,2},{2,1},{5,6},{6,5},{9,10},{10,9},{13,14},{14,13},{17,18},{18,... | collective-permute-start | bytes 24584 | tf_op jit(solution)/shard_map/ppermute | solution.py:384

commit v8 on v7

--- a/solution.py
+++ b/solution.py
@@ -144,7 +144,7 @@
 
 def prepare_kernel(
     step, full_ref, rank_ref, angle_ref, slope_ref, shift_ref,
-    lit_ref, size_ref, part_ref, coef_ref, cover_ref, flag_ref, gx_ref, pair, gy_ref,
+    lit_ref, size_ref, part_ref, coef_ref, cover_ref, flag_ref, gx_ref, order_ref, pair, gy_ref,
 ):
     dep, rows, cols = full_ref.shape
     slabs = rank_ref.shape[0]
@@ -159,6 +159,7 @@
     flag_ref[0] = jnp.sin(elevation)
     flag_ref[1] = jnp.full((SUB, cols), jnp.where(ascending, 1.0, 0.0), F32)
     flag_ref[2] = light_x
+    order_ref[0] = jnp.where(ascending, 1, 0)
 
     zero = jnp.zeros((PAD, 2 * cols), BF16)
     for p in range(2):
@@ -225,10 +226,10 @@
         lambda *refs: prepare_kernel(step, *refs),
         out_shape=(
             plane(dep), plane(dep), plane(dep), plane(3 * dep), pltpu.VMEM((rows, cols), F32),
-            pltpu.VMEM((3, SUB, cols), F32), plane(dep),
+            pltpu.VMEM((3, SUB, cols), F32), plane(dep), pltpu.SMEM((1,), jnp.int32),
         ),
         in_specs=[VMEM] + [SMEM] * 4,
-        out_specs=(VMEM,) * 7,
+        out_specs=(VMEM,) * 7 + (SMEM,),
         scratch_shapes=[
             pltpu.VMEM((2, rows + 2 * PAD, 2 * cols), BF16),
             pltpu.VMEM((2, BLK, 2 * cols), F32),
@@ -308,7 +309,7 @@
     start = 0
     for ref in (z1_ref,):
         body = functools.partial(group, start=start, z1_ref=ref)
-        lax.fori_loop(0, ref.shape[0], body, 0, unroll=8)
+        lax.fori_loop(0, ref.shape[0], body, 0, unroll=16)
         start += ref.shape[0]
 
 
@@ -327,11 +328,11 @@
     )(*(near(x) for x in (z1, z2, *ready)))
 
 
-def compose_kernel(part_ref, flag_ref, mean_ref, image_ref, out_ref, sem):
-    copy = pltpu.make_async_copy(mean_ref, out_ref, sem)
+def compose_kernel(part_ref, flag_ref, mean_ref, far_ref, out_ref, image_ref, sems):
+    copy = pltpu.make_async_copy(mean_ref, out_ref, sems.at[0])
     copy.start()
     slabs, _, cols = part_ref.shape
-    ascending = jnp.max(flag_ref[1, 0:8, :]) > 0.5
+    ascending = flag_ref[0] > 0
 
     def body(i, carry):
         through, red, green, blue = carry
@@ -349,7 +350,10 @@
     image_ref[1] = green
     image_ref[2] = blue
     image_ref[3] = 1.0 - through
+    last = pltpu.make_async_copy(image_ref, far_ref, sems.at[1])
+    last.start()
     copy.wait()
+    last.wait()
 
 
 def compose(parts, flag, mean):
@@ -359,12 +363,15 @@
             jax.ShapeDtypeStruct((4, 8, parts.shape[2]), F32),
             jax.ShapeDtypeStruct(mean.shape, F32),
         ),
-        in_specs=[VMEM] * 3,
-        out_specs=(VMEM, pl.BlockSpec(memory_space=pltpu.HBM)),
-        scratch_shapes=[pltpu.SemaphoreType.DMA],
+        in_specs=[VMEM, SMEM, VMEM],
+        out_specs=(pl.BlockSpec(memory_space=pltpu.HBM),) * 2,
+        scratch_shapes=[
+            pltpu.VMEM((4, 8, parts.shape[2]), F32),
+            pltpu.SemaphoreType.DMA((2,)),
+        ],
         compiler_params=GRANT,
         name="compose",
-    )(near(parts), near(flag), near(mean))
+    )(near(parts), pltpu.with_memory_space_constraint(flag, pltpu.SMEM), near(mean))
 
 
 def mates(count, start):
@@ -382,14 +389,14 @@
     z2 = lax.ppermute(z2, "depth", mates(slabs, 0))
     x1 = lax.ppermute(x1, "tile", mates(tiles, 0))
     x2 = lax.ppermute(x2, "tile", mates(tiles, 1))
-    *ready, gx = prepare(step, full, slab_rank, light_angles, color_slope, color_shift)
+    *ready, gx, forward = prepare(step, full, slab_rank, light_angles, color_slope, color_shift)
     ready[:2] = mend(*ready[:2], gx, ready[-1], x1, x2)
     image, mean = shade(z1, z2, ready)
     order = sorted(range(slabs), key=seat)
     parts = lax.all_to_all(
         image, "depth", split_axis=0, concat_axis=0, tiled=True, axis_index_groups=[order]
     )
-    return compose(parts, ready[-1], mean)
+    return compose(parts, forward, mean)
 
 
 def solution(mesh):

time: 53.4 us -> 53.2 us (level)
  no operation moved by 1% of the time
where the time goes in v8:
time: 53.2 us; the launch traced here: 53 us
  blocking collectives  26.8 us (50%)
  starting transfers between devices  13.8 us (26%)
  Pallas kernels  7.87 us (15%)
  waiting for transfers between devices  3.77 us (7%)
  between operations  0.69 us (1%)
    all_to_all x1, blocking collectives, shards(): lax.all_to_all(image, 'depth', split_axis=0, concat_axis=0, tiled=True, a...  26.8 us
    ppermute x1, starting transfers between devices, shards(): z2 = lax.ppermute(z2, 'depth', mates(slabs, 0))  9.33 us
    pallas_call x1, Pallas kernels, prepare(): pl.pallas_call(lambda *refs: prepare_kernel(step, *refs), out_shape=(plan...  3.29 us
    ppermute x1, waiting for transfers between devices, shards(): x2 = lax.ppermute(x2, 'tile', mates(tiles, 1))  3.02 us
    ppermute x1, starting transfers between devices, shards(): x2 = lax.ppermute(x2, 'tile', mates(tiles, 1))  2.52 us
    pallas_call x1, Pallas kernels, refine(): pl.pallas_call(refine_kernel, out_shape=(pltpu.VMEM((dep, rows, cols), BF...  1.6 us
    ppermute x1, starting transfers between devices, shards(): x1 = lax.ppermute(x1, 'tile', mates(tiles, 0))  1.26 us
    pallas_call x1, Pallas kernels, compose(): pl.pallas_call(compose_kernel, out_shape=(jax.ShapeDtypeStruct((4, 8, par...  1.12 us
  transfers between devices with their start and end apart: 4, of which 2 were waited for; matrix products, arithmetic and copies ran while one was open for 0% of the time, Pallas kernels for 8%

profile of v8, /device:TPU:1, one launch (start us, length us, event | category | flops | bytes accessed | tf_op | source)
XLA Modules:
  0.0 53.0 jit_solution(4982022524453324197)
XLA Ops:
  0.6 1.6 %refine.1 = (bf16[4,512,128]{2,1,0:T(8,128)(2,1)S(1)}, bf16[64,16,128]{2,1,0:T(8,128)(2,1)S(1)}, bf16[64,16,128]{2,1,0:T(8,128)(2,1)S(1)}) custom-call(bf16[4,512,128]{2,1,0:T(8,128)(2,1)} %res_ref.1, bf16[2,64,256]{2,1,0:T(8,128)(2,1)} %bitcast.4, s32[32,128]{1,0:T(8,128)} %bitcast.5), custom_call_target="tpu_custom_call" | custom-call | flops 100000000 | bytes 1000000 | tf_op jit(solution)/shard_map/refine/pallas_call | solution.py:134
  2.2 0.7 %collective-permute-start = (bf16[64,16,128]{2,1,0:T(8,128)(2,1)S(1)}, bf16[64,16,128]{2,1,0:T(8,128)(2,1)S(1)}, u32[]{:S(2)}, u32[]{:S(2)}) collective-permute-start(bf16[64,16,128]{2,1,0:T(8,128)(2,1)S(1)} %get-tuple-element.19), channel_id=1, source_target_pairs={{4,8},{12,16},{20,24},{28,32},{36,40},{44,48},{52,56},{60,64},{68,... | collective-permute-start | bytes 786440 | tf_op jit(solution)/shard_map/ppermute | solution.py:388
  2.9 9.3 %collective-permute-start.1 = (bf16[64,16,128]{2,1,0:T(8,128)(2,1)S(1)}, bf16[64,16,128]{2,1,0:T(8,128)(2,1)S(1)}, u32[]{:S(2)}, u32[]{:S(2)}) collective-permute-start(bf16[64,16,128]{2,1,0:T(8,128)(2,1)S(1)} %get-tuple-element.20), channel_id=1, source_target_pairs={{0,4},{8,12},{16,20},{24,28},{32,36},{40,44},{48,52},{56,60},{64,6... | collective-permute-start | bytes 786440 | tf_op jit(solution)/shard_map/ppermute | solution.py:389
  12.2 0.2 columns.1
  12.5 1.3 %collective-permute-start.2 = (bf16[8,512]{1,0:T(8,128)(2,1)S(1)}, bf16[8,512]{1,0:T(8,128)(2,1)S(1)}, u32[]{:S(2)}, u32[]{:S(2)}) collective-permute-start(bf16[8,512]{1,0:T(8,128)(2,1)S(1)} %get-tuple-element.26), channel_id=1, source_target_pairs={{0,1},{2,3},{1,0},{3,2},{4,5},{6,7},{5,4},{7,6},{8,9},{10,11},{9,8... | collective-permute-start | bytes 24584 | tf_op jit(solution)/shard_map/ppermute | solution.py:390
  13.7 2.5 %collective-permute-start.3 = (bf16[8,512]{1,0:T(8,128)(2,1)S(1)}, bf16[8,512]{1,0:T(8,128)(2,1)S(1)}, u32[]{:S(2)}, u32[]{:S(2)}) collective-permute-start(bf16[8,512]{1,0:T(8,128)(2,1)S(1)} %get-tuple-element.27), channel_id=1, source_target_pairs={{1,2},{2,1},{5,6},{6,5},{9,10},{10,9},{13,14},{14,13},{17,18},{18,... | collective-permute-start | bytes 24584 | tf_op jit(solution)/shard_map/ppermute | solution.py:391
  16.3 3.3 %prepare.1 = (f32[4,512,128]{2,1,0:T(8,128)S(1)}, f32[4,512,128]{2,1,0:T(8,128)S(1)}, f32[4,512,128]{2,1,0:T(8,128)S(1)}, f32[12,512,128]{2,1,0:T(8,128)S(1)}, f...) custom-call(bf16[4,512,128]{2,1,0:T(8,128)(2,1)S(1)} %get-tuple-element.21.refs_0_, ...), custom_call_target="tpu_custom_call" | custom-call | flops 1000000000 | bytes 1000000 | tf_op jit(solution)/shard_map/prepare/pallas_call | solution.py:225
  19.6 0.0 collective-permute-done.2.x1_ref
  19.6 3.0 %collective-permute-done.3.x2_ref = bf16[8,512]{1,0:T(8,128)(2,1)S(1)} collective-permute-done((bf16[8,512]{1,0:T(8,128)(2,1)S(1)}, bf16[8,512]{1,0:T(8,128)(2,1)S(1)}, u32[]{:S(2)}, u32[]{:S(2)}) %collective-permute-start.3) | collective-permute-done | bytes 8224 | tf_op jit(solution)/shard_map/ppermute | solution.py:391
  22.6 0.8 %mend.1 = (f32[4,512,128]{2,1,0:T(8,128)S(1)}, f32[4,512,128]{2,1,0:T(8,128)S(1)}) custom-call(f32[4,512,128]{2,1,0:T(8,128)S(1)} %get-tuple-element.22.lit_ref, f32[4,512,128]{2,1,0:T(8,128)S(1)} %get-tuple-element.23.size_ref, f32[4,512,128]{2,1,0:T(8,128)S(1)} %get-tuple-element.24.gx_ref, ...), custom_call_target="tpu_custom_call", output_to_operand_aliasing={{0}: (0, {}), {1}: (1, {})} | custom-call | flops 100000000 | bytes 1000000 | tf_op jit(solution)/shard_map/mend/pallas_call | solution.py:262
  23.4 0.0 collective-permute-done.z1_ref
  23.4 0.7 %collective-permute-done.1.z2_ref = bf16[64,16,128]{2,1,0:T(8,128)(2,1)S(1)} collective-permute-done((bf16[64,16,128]{2,1,0:T(8,128)(2,1)S(1)}, bf16[64,16,128]{2,1,0:T(8,128)(2,1)S(1)}, u32[]{:S(2)}, u32[]{:S(2)}) %collective-permute-start.1) | collective-permute-done | bytes 262176 | tf_op jit(solution)/shard_map/ppermute | solution.py:389
  24.2 0.8 %shade.1 = (bf16[64,32,128]{2,1,0:T(8,128)(2,1)S(1)}, f32[1,512,128]{2,1,0:T(8,128)S(1)}) custom-call(bf16[64,16,128]{2,1,0:T(8,128)(2,1)S(1)} %collective-permute-done.z1_ref, bf16[64,16,128]{2,1,0:T(8,128)(2,1)S(1)} %collective-permute-done.1.z2_ref, f32[4,512,128]{2,1,0:T(8,128)S(1)} %get-tuple-element.28.lit_ref, ...), custom_call_target="tpu_custom_call" | custom-call | tf_op jit(solution)/shard_map/shade/pallas_call | solution.py:318
  25.0 26.8 %all_to_all.5.part_ref = bf16[64,32,128]{2,1,0:T(8,128)(2,1)S(1)} all-to-all(bf16[64,32,128]{2,1,0:T(8,128)(2,1)S(1)} %get-tuple-element.33), channel_id=1, replica_groups={{252,236,220,204,188,172,156,140,124,108,92,76,60,44,28,12,248,232,216,..., dimensions={0} | all-to-all | bytes 1048576 | tf_op jit(solution)/shard_map/all_to_all | solution.py:396
  51.8 1.1 %compose.1 = (f32[4,8,128]{2,1,0:T(8,128)}, f32[1,512,128]{2,1,0:T(8,128)}) custom-call(bf16[64,32,128]{2,1,0:T(8,128)(2,1)S(1)} %all_to_all.5.part_ref, s32[1]{0:T(128)S(4)} %get-tuple-element.34.flag_ref, f32[1,512,128]{2,1,0:T(8,128)S(1)} %get-tuple-element.35.mean_ref), custom_call_target="tpu_custom_call" | custom-call | tf_op jit(solution)/shard_map/compose/pallas_call | solution.py:360
Async XLA Ops:
  2.2 21.2 %collective-permute-start = (bf16[64,16,128]{2,1,0:T(8,128)(2,1)S(1)}, bf16[64,16,128]{2,1,0:T(8,128)(2,1)S(1)}, u32[]{:S(2)}, u32[]{:S(2)}) collective-permute-start(bf16[64,16,128]{2,1,0:T(8,128)(2,1)S(1)} %get-tuple-element.19), channel_id=1, source_target_pairs={{4,8},{12,16},{20,24},{28,32},{36,40},{44,48},{52,56},{60,64},{68,... | collective-permute-start | bytes 786440 | tf_op jit(solution)/shard_map/ppermute | solution.py:388
  2.9 21.2 %collective-permute-start.1 = (bf16[64,16,128]{2,1,0:T(8,128)(2,1)S(1)}, bf16[64,16,128]{2,1,0:T(8,128)(2,1)S(1)}, u32[]{:S(2)}, u32[]{:S(2)}) collective-permute-start(bf16[64,16,128]{2,1,0:T(8,128)(2,1)S(1)} %get-tuple-element.20), channel_id=1, source_target_pairs={{0,4},{8,12},{16,20},{24,28},{32,36},{40,44},{48,52},{56,60},{64,6... | collective-permute-start | bytes 786440 | tf_op jit(solution)/shard_map/ppermute | solution.py:389
  12.5 7.1 %collective-permute-start.2 = (bf16[8,512]{1,0:T(8,128)(2,1)S(1)}, bf16[8,512]{1,0:T(8,128)(2,1)S(1)}, u32[]{:S(2)}, u32[]{:S(2)}) collective-permute-start(bf16[8,512]{1,0:T(8,128)(2,1)S(1)} %get-tuple-element.26), channel_id=1, source_target_pairs={{0,1},{2,3},{1,0},{3,2},{4,5},{6,7},{5,4},{7,6},{8,9},{10,11},{9,8... | collective-permute-start | bytes 24584 | tf_op jit(solution)/shard_map/ppermute | solution.py:390
  13.7 8.9 %collective-permute-start.3 = (bf16[8,512]{1,0:T(8,128)(2,1)S(1)}, bf16[8,512]{1,0:T(8,128)(2,1)S(1)}, u32[]{:S(2)}, u32[]{:S(2)}) collective-permute-start(bf16[8,512]{1,0:T(8,128)(2,1)S(1)} %get-tuple-element.27), channel_id=1, source_target_pairs={{1,2},{2,1},{5,6},{6,5},{9,10},{10,9},{13,14},{14,13},{17,18},{18,... | collective-permute-start | bytes 24584 | tf_op jit(solution)/shard_map/ppermute | solution.py:391

commit v9 on v8

--- a/solution.py
+++ b/solution.py
@@ -210,7 +210,7 @@
                 jnp.where(ascending, up[3], 1.0),
             ]
             for z in range(4):
-                weight = before[z] * (1.0 - clear[z]) * visible
+                weight = before[z] * (1.0 - clear[z]) * (0.75 * visible)
                 for n in range(3):
                     coef_ref[3 * z + n, row, :] = weight * color[z][n]
             cover_ref[row, :] = encode((1.0 - up[3] * clear[3]) * visible)
@@ -296,14 +296,14 @@
         for z in range(4):
             lit = lit_ref[z, row, :] + light_z * gz[z]
             size = size_ref[z, row, :] + gz[z] * gz[z]
-            shade.append(0.25 + 0.75 * (jnp.abs(lit) * lax.rsqrt(size)))
+            shade.append(jnp.abs(lit) * lax.rsqrt(size) + 1.0 / 3.0)
         out = []
         for n in range(3):
             p = [shade[z] * coef_ref[3 * z + n, row, :] for z in range(4)]
             out.append(encode((p[0] + p[1]) + (p[2] + p[3])))
         out.append(cover_ref[row, :])
         image_ref[seat(r)] = jnp.concatenate(out, 0).astype(BF16)
-        mean_ref[0, row, :] = 0.25 * ((shade[0] + shade[1]) + (shade[2] + shade[3]))
+        mean_ref[0, row, :] = 0.1875 * ((shade[0] + shade[1]) + (shade[2] + shade[3]))
         return carry
 
     start = 0

time: 53.2 us -> 53.2 us (level)
  no operation moved by 1% of the time
where the time goes in v9:
time: 53.2 us; the launch traced here: 53 us
  blocking collectives  26.8 us (50%)
  starting transfers between devices  13.8 us (26%)
  Pallas kernels  7.89 us (15%)
  waiting for transfers between devices  3.77 us (7%)
  between operations  0.69 us (1%)
    all_to_all x1, blocking collectives, shards(): lax.all_to_all(image, 'depth', split_axis=0, concat_axis=0, tiled=True, a...  26.8 us
    ppermute x1, starting transfers between devices, shards(): z2 = lax.ppermute(z2, 'depth', mates(slabs, 0))  9.33 us
    pallas_call x1, Pallas kernels, prepare(): pl.pallas_call(lambda *refs: prepare_kernel(step, *refs), out_shape=(plan...  3.3 us
    ppermute x1, waiting for transfers between devices, shards(): x2 = lax.ppermute(x2, 'tile', mates(tiles, 1))  3.01 us
    ppermute x1, starting transfers between devices, shards(): x2 = lax.ppermute(x2, 'tile', mates(tiles, 1))  2.52 us
    pallas_call x1, Pallas kernels, refine(): pl.pallas_call(refine_kernel, out_shape=(pltpu.VMEM((dep, rows, cols), BF...  1.6 us
    ppermute x1, starting transfers between devices, shards(): x1 = lax.ppermute(x1, 'tile', mates(tiles, 0))  1.26 us
    pallas_call x1, Pallas kernels, compose(): pl.pallas_call(compose_kernel, out_shape=(jax.ShapeDtypeStruct((4, 8, par...  1.12 us
  transfers between devices with their start and end apart: 4, of which 2 were waited for; matrix products, arithmetic and copies ran while one was open for 0% of the time, Pallas kernels for 8%

profile of v9, /device:TPU:1, one launch (start us, length us, event | category | flops | bytes accessed | tf_op | source)
XLA Modules:
  0.0 53.0 jit_solution(4065383443179111923)
XLA Ops:
  0.6 1.6 %refine.1 = (bf16[4,512,128]{2,1,0:T(8,128)(2,1)S(1)}, bf16[64,16,128]{2,1,0:T(8,128)(2,1)S(1)}, bf16[64,16,128]{2,1,0:T(8,128)(2,1)S(1)}) custom-call(bf16[4,512,128]{2,1,0:T(8,128)(2,1)} %res_ref.1, bf16[2,64,256]{2,1,0:T(8,128)(2,1)} %bitcast.4, s32[32,128]{1,0:T(8,128)} %bitcast.5), custom_call_target="tpu_custom_call" | custom-call | flops 100000000 | bytes 1000000 | tf_op jit(solution)/shard_map/refine/pallas_call | solution.py:134
  2.2 0.7 %collective-permute-start = (bf16[64,16,128]{2,1,0:T(8,128)(2,1)S(1)}, bf16[64,16,128]{2,1,0:T(8,128)(2,1)S(1)}, u32[]{:S(2)}, u32[]{:S(2)}) collective-permute-start(bf16[64,16,128]{2,1,0:T(8,128)(2,1)S(1)} %get-tuple-element.19), channel_id=1, source_target_pairs={{4,8},{12,16},{20,24},{28,32},{36,40},{44,48},{52,56},{60,64},{68,... | collective-permute-start | bytes 786440 | tf_op jit(solution)/shard_map/ppermute | solution.py:388
  2.9 9.3 %collective-permute-start.1 = (bf16[64,16,128]{2,1,0:T(8,128)(2,1)S(1)}, bf16[64,16,128]{2,1,0:T(8,128)(2,1)S(1)}, u32[]{:S(2)}, u32[]{:S(2)}) collective-permute-start(bf16[64,16,128]{2,1,0:T(8,128)(2,1)S(1)} %get-tuple-element.20), channel_id=1, source_target_pairs={{0,4},{8,12},{16,20},{24,28},{32,36},{40,44},{48,52},{56,60},{64,6... | collective-permute-start | bytes 786440 | tf_op jit(solution)/shard_map/ppermute | solution.py:389
  12.2 0.2 columns.1
  12.5 1.3 %collective-permute-start.2 = (bf16[8,512]{1,0:T(8,128)(2,1)S(1)}, bf16[8,512]{1,0:T(8,128)(2,1)S(1)}, u32[]{:S(2)}, u32[]{:S(2)}) collective-permute-start(bf16[8,512]{1,0:T(8,128)(2,1)S(1)} %get-tuple-element.26), channel_id=1, source_target_pairs={{0,1},{2,3},{1,0},{3,2},{4,5},{6,7},{5,4},{7,6},{8,9},{10,11},{9,8... | collective-permute-start | bytes 24584 | tf_op jit(solution)/shard_map/ppermute | solution.py:390
  13.7 2.5 %collective-permute-start.3 = (bf16[8,512]{1,0:T(8,128)(2,1)S(1)}, bf16[8,512]{1,0:T(8,128)(2,1)S(1)}, u32[]{:S(2)}, u32[]{:S(2)}) collective-permute-start(bf16[8,512]{1,0:T(8,128)(2,1)S(1)} %get-tuple-element.27), channel_id=1, source_target_pairs={{1,2},{2,1},{5,6},{6,5},{9,10},{10,9},{13,14},{14,13},{17,18},{18,... | collective-permute-start | bytes 24584 | tf_op jit(solution)/shard_map/ppermute | solution.py:391
  16.3 3.3 %prepare.1 = (f32[4,512,128]{2,1,0:T(8,128)S(1)}, f32[4,512,128]{2,1,0:T(8,128)S(1)}, f32[4,512,128]{2,1,0:T(8,128)S(1)}, f32[12,512,128]{2,1,0:T(8,128)S(1)}, f...) custom-call(bf16[4,512,128]{2,1,0:T(8,128)(2,1)S(1)} %get-tuple-element.21.refs_0_, ...), custom_call_target="tpu_custom_call" | custom-call | flops 1000000000 | bytes 1000000 | tf_op jit(solution)/shard_map/prepare/pallas_call | solution.py:225
  19.6 0.0 collective-permute-done.2.x1_ref
  19.6 3.0 %collective-permute-done.3.x2_ref = bf16[8,512]{1,0:T(8,128)(2,1)S(1)} collective-permute-done((bf16[8,512]{1,0:T(8,128)(2,1)S(1)}, bf16[8,512]{1,0:T(8,128)(2,1)S(1)}, u32[]{:S(2)}, u32[]{:S(2)}) %collective-permute-start.3) | collective-permute-done | bytes 8224 | tf_op jit(solution)/shard_map/ppermute | solution.py:391
  22.6 0.8 %mend.1 = (f32[4,512,128]{2,1,0:T(8,128)S(1)}, f32[4,512,128]{2,1,0:T(8,128)S(1)}) custom-call(f32[4,512,128]{2,1,0:T(8,128)S(1)} %get-tuple-element.22.lit_ref, f32[4,512,128]{2,1,0:T(8,128)S(1)} %get-tuple-element.23.size_ref, f32[4,512,128]{2,1,0:T(8,128)S(1)} %get-tuple-element.24.gx_ref, ...), custom_call_target="tpu_custom_call", output_to_operand_aliasing={{0}: (0, {}), {1}: (1, {})} | custom-call | flops 100000000 | bytes 1000000 | tf_op jit(solution)/shard_map/mend/pallas_call | solution.py:262
  23.4 0.0 collective-permute-done.z1_ref
  23.4 0.7 %collective-permute-done.1.z2_ref = bf16[64,16,128]{2,1,0:T(8,128)(2,1)S(1)} collective-permute-done((bf16[64,16,128]{2,1,0:T(8,128)(2,1)S(1)}, bf16[64,16,128]{2,1,0:T(8,128)(2,1)S(1)}, u32[]{:S(2)}, u32[]{:S(2)}) %collective-permute-start.1) | collective-permute-done | bytes 262176 | tf_op jit(solution)/shard_map/ppermute | solution.py:389
  24.2 0.8 %shade.1 = (bf16[64,32,128]{2,1,0:T(8,128)(2,1)S(1)}, f32[1,512,128]{2,1,0:T(8,128)S(1)}) custom-call(bf16[64,16,128]{2,1,0:T(8,128)(2,1)S(1)} %collective-permute-done.z1_ref, bf16[64,16,128]{2,1,0:T(8,128)(2,1)S(1)} %collective-permute-done.1.z2_ref, f32[4,512,128]{2,1,0:T(8,128)S(1)} %get-tuple-element.28.lit_ref, ...), custom_call_target="tpu_custom_call" | custom-call | tf_op jit(solution)/shard_map/shade/pallas_call | solution.py:318
  25.0 26.8 %all_to_all.5.part_ref = bf16[64,32,128]{2,1,0:T(8,128)(2,1)S(1)} all-to-all(bf16[64,32,128]{2,1,0:T(8,128)(2,1)S(1)} %get-tuple-element.33), channel_id=1, replica_groups={{252,236,220,204,188,172,156,140,124,108,92,76,60,44,28,12,248,232,216,..., dimensions={0} | all-to-all | bytes 1048576 | tf_op jit(solution)/shard_map/all_to_all | solution.py:396
  51.8 1.1 %compose.1 = (f32[4,8,128]{2,1,0:T(8,128)}, f32[1,512,128]{2,1,0:T(8,128)}) custom-call(bf16[64,32,128]{2,1,0:T(8,128)(2,1)S(1)} %all_to_all.5.part_ref, s32[1]{0:T(128)S(4)} %get-tuple-element.34.flag_ref, f32[1,512,128]{2,1,0:T(8,128)S(1)} %get-tuple-element.35.mean_ref), custom_call_target="tpu_custom_call" | custom-call | tf_op jit(solution)/shard_map/compose/pallas_call | solution.py:360
Async XLA Ops:
  2.2 21.2 %collective-permute-start = (bf16[64,16,128]{2,1,0:T(8,128)(2,1)S(1)}, bf16[64,16,128]{2,1,0:T(8,128)(2,1)S(1)}, u32[]{:S(2)}, u32[]{:S(2)}) collective-permute-start(bf16[64,16,128]{2,1,0:T(8,128)(2,1)S(1)} %get-tuple-element.19), channel_id=1, source_target_pairs={{4,8},{12,16},{20,24},{28,32},{36,40},{44,48},{52,56},{60,64},{68,... | collective-permute-start | bytes 786440 | tf_op jit(solution)/shard_map/ppermute | solution.py:388
  2.9 21.2 %collective-permute-start.1 = (bf16[64,16,128]{2,1,0:T(8,128)(2,1)S(1)}, bf16[64,16,128]{2,1,0:T(8,128)(2,1)S(1)}, u32[]{:S(2)}, u32[]{:S(2)}) collective-permute-start(bf16[64,16,128]{2,1,0:T(8,128)(2,1)S(1)} %get-tuple-element.20), channel_id=1, source_target_pairs={{0,4},{8,12},{16,20},{24,28},{32,36},{40,44},{48,52},{56,60},{64,6... | collective-permute-start | bytes 786440 | tf_op jit(solution)/shard_map/ppermute | solution.py:389
  12.5 7.1 %collective-permute-start.2 = (bf16[8,512]{1,0:T(8,128)(2,1)S(1)}, bf16[8,512]{1,0:T(8,128)(2,1)S(1)}, u32[]{:S(2)}, u32[]{:S(2)}) collective-permute-start(bf16[8,512]{1,0:T(8,128)(2,1)S(1)} %get-tuple-element.26), channel_id=1, source_target_pairs={{0,1},{2,3},{1,0},{3,2},{4,5},{6,7},{5,4},{7,6},{8,9},{10,11},{9,8... | collective-permute-start | bytes 24584 | tf_op jit(solution)/shard_map/ppermute | solution.py:390
  13.7 8.9 %collective-permute-start.3 = (bf16[8,512]{1,0:T(8,128)(2,1)S(1)}, bf16[8,512]{1,0:T(8,128)(2,1)S(1)}, u32[]{:S(2)}, u32[]{:S(2)}) collective-permute-start(bf16[8,512]{1,0:T(8,128)(2,1)S(1)} %get-tuple-element.27), channel_id=1, source_target_pairs={{1,2},{2,1},{5,6},{6,5},{9,10},{10,9},{13,14},{14,13},{17,18},{18,... | collective-permute-start | bytes 24584 | tf_op jit(solution)/shard_map/ppermute | solution.py:391
